TPU v7x, 32 devices: a 4x2x2 block of a 4x4x8 slice. The times are simulated.
32 devices in a mesh: data: 4 (over y, z), dap: 8 (over x, core).
Axes of the slice: x: 4, y: 2, z: 2, core: 2. Of those that a mesh axis runs over, the one named last changes fastest.
The devices are a block of a 4x4x8 slice.
Arguments:
- pair_act: float32 [1024, 256, 128], P(('data', 'dap')), parts along dimension 0
- pair_mask: int32 [1024, 256], P(('data', 'dap')), parts along dimension 0
- msa_act: bfloat16 [512, 1024, 256], P(None, ('data', 'dap')), parts along dimension 1
- opm_norm: float32 [2, 256], replicated
- opm_proj: bfloat16 [256, 64], replicated
- opm_out: bfloat16 [1024, 128], replicated
- opm_bias: float32 [128], replicated
- tri_norm: float32 [2, 2, 128], replicated
- tri_proj: bfloat16 [2, 128, 512], replicated
- tri_gate: bfloat16 [2, 128, 128], replicated
- tri_xnorm: float32 [2, 2, 128], replicated
- tri_out: bfloat16 [2, 128, 128], replicated
Outputs:
- output: float32 [1024, 256, 128], P(('data', 'dap')), parts along dimension 0
There are 4 independent parts. A program takes and returns all parts, laid end to end along the dimension named above; an argument that names none is the same for every part.
All inputs are finite; a program needn't handle non-finite values.
Results may differ from a plain program's by a relative error of at most 0.00337041.
Values are sent between devices in bfloat16 or wider.
A program may use at most 768 MiB of HBM per device.

v0:
```python
import jax
import jax.numpy as jnp
from jax import lax
from jax.sharding import PartitionSpec as P

LN_EPS = 1e-5


def norm_over(values, norm_scale, norm_shift, norm_axis):
    chan_mean = jnp.mean(values, axis=norm_axis, keepdims=True)
    centered = values - chan_mean
    chan_var = jnp.mean(centered * centered, axis=norm_axis, keepdims=True)
    return (centered * lax.rsqrt(chan_var + LN_EPS) * norm_scale + norm_shift).astype(jnp.bfloat16)


def gated_act(proj_vals, mask_f, tri_dim):
    return (mask_f * jax.nn.sigmoid(proj_vals[tri_dim:]) * proj_vals[:tri_dim]).astype(jnp.bfloat16)


def outer_product_mean(value_a7, opm_norm, opm_proj, opm_out, opm_bias):
    value_a9 = value_a7.shape[0]
    opm_dim = opm_proj.shape[1] // 2
    value_a8 = norm_over(value_a7.astype(jnp.float32), opm_norm[0], opm_norm[1], -1)
    proj_all = jnp.einsum("srm,mp->srp", value_a8, opm_proj, preferred_element_type=jnp.float32).astype(jnp.bfloat16)
    right_full = lax.all_gather(proj_all[:, :, opm_dim:], "dap", axis=1, tiled=True)
    outer_prod = jnp.einsum("sip,sjq->ijpq", proj_all[:, :, :opm_dim], right_full, preferred_element_type=jnp.float32) / value_a9
    local_rows = outer_prod.shape[0]
    residues = outer_prod.shape[1]
    outer_flat = outer_prod.astype(jnp.bfloat16).reshape(local_rows, residues, opm_dim * opm_dim)
    return jnp.einsum("ijf,fz->ijz", outer_flat, opm_out, preferred_element_type=jnp.float32) + opm_bias


def triangle_update(pair_loc, mask_f, norm_pair, w_proj, w_gate, norm_mix, w_out, incoming):
    tri_dim = w_out.shape[0]
    pair_norm = norm_over(pair_loc, norm_pair[0], norm_pair[1], -1)
    proj_all = jnp.einsum("zc,rnz->crn", w_proj, pair_norm, preferred_element_type=jnp.float32)
    left_act = gated_act(proj_all[:2 * tri_dim], mask_f, tri_dim)
    right_act = gated_act(proj_all[2 * tri_dim:], mask_f, tri_dim)
    left_chan = lax.all_to_all(left_act, "dap", 0, 1, tiled=True)
    right_chan = lax.all_to_all(right_act, "dap", 0, 1, tiled=True)
    einsum_form = "cki,ckj->cij" if incoming else "cik,cjk->cij"
    mixed_chan = jnp.einsum(einsum_form, left_chan, right_chan, preferred_element_type=jnp.float32).astype(jnp.bfloat16)
    mixed_rows = lax.all_to_all(mixed_chan, "dap", 1, 0, tiled=True)
    mixed_norm = norm_over(mixed_rows.astype(jnp.float32), norm_mix[0][:, None, None], norm_mix[1][:, None, None], 0)
    gate_act = jax.nn.sigmoid(jnp.einsum("rnz,zy->rny", pair_norm, w_gate, preferred_element_type=jnp.float32))
    update = jnp.einsum("crn,cz->rnz", mixed_norm, w_out, preferred_element_type=jnp.float32)
    return pair_loc + gate_act * update


def solution(mesh):
    row_spec = P(("data", "dap"), None, None)
    mask_spec = P(("data", "dap"), None)
    array_b8 = P(None, ("data", "dap"), None)
    replicated = P()

    def local_program(pair_loc, mask_loc, value_a7, opm_norm, opm_proj, opm_out, opm_bias, tri_norm, tri_proj, tri_gate, tri_xnorm, tri_out):
        mask_f = mask_loc.astype(jnp.float32)[None]
        pair_zero = pair_loc + outer_product_mean(value_a7, opm_norm, opm_proj, opm_out, opm_bias)
        pair_one = triangle_update(pair_zero, mask_f, tri_norm[0], tri_proj[0], tri_gate[0], tri_xnorm[0], tri_out[0], False)
        return triangle_update(pair_one, mask_f, tri_norm[1], tri_proj[1], tri_gate[1], tri_xnorm[1], tri_out[1], True)

    return jax.shard_map(local_program, mesh=mesh, in_specs=(row_spec, mask_spec, array_b8) + (replicated,) * 9, out_specs=row_spec, check_vma=False)
```

profile of v0, /device:TPU:81, one launch (start us, length us, event | category | flops | bytes accessed | tf_op | source)
XLA Modules:
  0.0 383.2 jit_solution(5733315734895115461)
XLA Ops:
  6.6 5.8 %convert_reduce_fusion = f32[512,32]{1,0:T(8,128)S(1)} fusion(bf16[512,32,256]{2,1,0:T(8,128)(2,1)} %param.14), kind=kLoop, calls=%fused_computation.2 | loop fusion | flops 8372224 | bytes 8454144 | tf_op jit(solution)/shard_map/reduce_sum | solution.py:10
  12.4 14.0 %fusion.2 = f32[512,32]{1,0:T(8,128)S(1)} fusion(bf16[512,32,256]{2,1,0:T(8,128)(2,1)S(1)} %copy-done.4, f32[512,32]{1,0:T(8,128)S(1)} %broadcast_multiply_fusion), kind=kLoop, calls=%fused_computation.5 | loop fusion | flops 16760832 | bytes 8519680 | tf_op jit(solution)/shard_map/reduce_sum | solution.py:12
  26.4 7.3 %fusion.5 = bf16[512,32,256]{2,1,0:T(8,128)(2,1)S(1)} fusion(bf16[512,32,256]{2,1,0:T(8,128)(2,1)S(1)} %copy-done.4, f32[256]{0:T(256)S(1)} %bitcast.135, f32[256]{0:T(256)S(1)} %bitcast.134, f32[512,32]{1,0:T(8,128)S(1)} %add_rsqrt_fusion, f32[512,32]{1,0:T(8,128)S(1)} %broadcast_multiply_fusion), kind=kLoop, calls=%fused_computation.8 | loop fusion | flops 25165824 | bytes 16910336 | tf_op jit(solution)/shard_map/convert_element_type | solution.py:13
  33.7 9.3 %fusion.47 = bf16[512,32,64]{0,2,1:T(8,128)(2,1)S(1)} fusion(bf16[512,32,256]{2,1,0:T(8,128)(2,1)S(1)} %fusion.5, bf16[256,64]{0,1:T(8,128)(2,1)S(1)} %copy-done.18), kind=kOutput, calls=%fused_computation.69 | convolution fusion | flops 537919488 | bytes 10518528 | tf_op jit(solution)/shard_map/srm,mp->srp/dot_general | solution.py:24
  43.1 1.1 slice.136
  44.2 6.1 %copy.98 = f32[32,256,128]{1,2,0:T(8,128)} copy(f32[32,256,128]{2,1,0:T(8,128)} %param.12) | data formatting | bytes 8388608 | tf_op args[0]
  50.4 44.9 %all-gather.2.cloned.1.call-done = bf16[512,256,32]{0,2,1:T(8,128)(2,1)} async-done(((bf16[512,32,32]{0,2,1:T(8,128)(2,1)}), bf16[512,256,32]{0,2,1:T(8,128)(2,1)}) %all-gather.2.cloned.1.call-update) | async-done | bytes 8388624 | tf_op jit(solution)/shard_map/all_gather | solution.py:25
  95.3 19.7 %fusion.6 = bf16[32,256,32,32]{1,2,0,3:T(8,128)(2,1)} fusion(bf16[512,256,32,1]{0,2,1,3:T(8,128)(2,1)} %bitcast.136, bf16[512,32,64]{0,2,1:T(8,128)(2,1)S(1)} %fusion.47), kind=kOutput, calls=%fused_computation.9 | convolution fusion | flops 8606711808 | bytes 26214400 | tf_op jit(solution)/shard_map/sip,sjq->ijpq/dot_general | solution.py:26
  115.0 16.2 %copy.95 = bf16[32,256,32,32]{1,3,2,0:T(8,128)(2,1)S(1)} copy(bf16[32,256,32,32]{1,2,0,3:T(8,128)(2,1)} %fusion.6) | data formatting | bytes 33554432 | tf_op jit(solution)/shard_map/convert_element_type | solution.py:29
  131.2 3.2 fusion.67
  135.6 2.6 convolution_bitcast_fusion.1
  138.2 3.5 fusion.20
  141.6 4.6 %copy.102 = bf16[128,32,256]{2,1,0:T(8,128)(2,1)} copy(bf16[128,32,256]{0,2,1:T(8,128)(2,1)} %get-tuple-element.12) | data formatting | bytes 4194304 | tf_op jit(solution)/shard_map/convert_element_type | solution.py:17
  146.2 4.5 %all-to-all-start = ((bf16[128,32,256]{2,1,0:T(8,128)(2,1)}), bf16[128,32,256]{2,1,0:T(8,128)(2,1)}, u32[]{:S(2)}, u32[]{:S(2)}) async-start(bf16[128,32,256]{2,1,0:T(8,128)(2,1)} %copy.102), calls=%async_computation | async-start | bytes 4194304 | tf_op jit(solution)/shard_map/all_to_all | solution.py:39
  150.7 3.0 copy.104
  153.7 23.2 %all-to-all-done = bf16[128,32,256]{2,1,0:T(8,128)(2,1)} async-done(((bf16[128,32,256]{2,1,0:T(8,128)(2,1)}), bf16[128,32,256]{2,1,0:T(8,128)(2,1)}, u32[]{:S(2)}, u32[]{:S(2)}) %all-to-all-start) | async-done | bytes 2097184 | tf_op jit(solution)/shard_map/all_to_all | solution.py:39
  176.9 5.3 %all-to-all-start.1 = ((bf16[128,32,256]{2,1,0:T(8,128)(2,1)}), bf16[128,32,256]{2,1,0:T(8,128)(2,1)}, u32[]{:S(2)}, u32[]{:S(2)}) async-start(bf16[128,32,256]{2,1,0:T(8,128)(2,1)} %copy.104), calls=%async_computation.1 | async-start | bytes 4194304 | tf_op jit(solution)/shard_map/all_to_all | solution.py:40
  182.2 1.8 copy.103
  184.0 24.4 %all-to-all-done.1 = bf16[128,32,256]{2,1,0:T(8,128)(2,1)} async-done(((bf16[128,32,256]{2,1,0:T(8,128)(2,1)}), bf16[128,32,256]{2,1,0:T(8,128)(2,1)}, u32[]{:S(2)}, u32[]{:S(2)}) %all-to-all-start.1) | async-done | bytes 2097184 | tf_op jit(solution)/shard_map/all_to_all | solution.py:40
  208.4 1.8 copy.105
  211.0 2.5 copy.106
  213.5 4.9 %all-to-all-start.2 = ((bf16[16,256,256]{2,0,1:T(8,128)(2,1)}), bf16[16,256,256]{2,0,1:T(8,128)(2,1)S(1)}, u32[]{:S(2)}, u32[]{:S(2)}) async-start(bf16[16,256,256]{2,0,1:T(8,128)(2,1)} %copy.106), calls=%async_computation.2 | async-start | bytes 4194304 | tf_op jit(solution)/shard_map/all_to_all | solution.py:43
  218.6 5.0 %fusion.56 = f32[32,256,128]{1,2,0:T(8,128)} fusion(bf16[2,128,128]{2,1,0:T(8,128)(2,1)S(1)} %copy-done.11, f32[32,256,128]{1,2,0:T(8,128)} %copy-done.2, f32[128]{0:T(128)S(1)} %get-tuple-element.14, f32[128]{0:T(128)S(1)} %get-tuple-element.15, f32[32,256]{1,0:T(8,128)S(1)} %add_rsqrt_fusion.4, f32[32,256]{1,0:T(8,128)S(1)} %broadcast_multiply_fusion.4), kind=kOutput, calls=%fused_computation.81 | convolution fusion | flops 273678336 | bytes 8487936 | tf_op jit(solution)/shard_map/rnz,zy->rny/dot_general | solution.py:45
  223.6 20.8 %all-to-all-done.2 = bf16[16,256,256]{2,0,1:T(8,128)(2,1)S(1)} async-done(((bf16[16,256,256]{2,0,1:T(8,128)(2,1)}), bf16[16,256,256]{2,0,1:T(8,128)(2,1)S(1)}, u32[]{:S(2)}, u32[]{:S(2)}) %all-to-all-start.2) | async-done | bytes 2097184 | tf_op jit(solution)/shard_map/all_to_all | solution.py:43
  245.4 0.9 fusion.45
  246.6 1.0 copy-done.3
  247.6 1.3 copy-done.8
  248.9 1.7 fusion.68
  251.3 2.7 convolution_bitcast_fusion
  254.0 3.5 fusion.10
  257.4 4.6 %copy.112 = bf16[128,32,256]{2,1,0:T(8,128)(2,1)} copy(bf16[128,32,256]{0,2,1:T(8,128)(2,1)} %get-tuple-element.10) | data formatting | bytes 4194304 | tf_op jit(solution)/shard_map/convert_element_type | solution.py:17
  262.0 5.4 %all-to-all-start.3 = ((bf16[128,32,256]{2,1,0:T(8,128)(2,1)}), bf16[128,32,256]{2,1,0:T(8,128)(2,1)}, u32[]{:S(2)}, u32[]{:S(2)}) async-start(bf16[128,32,256]{2,1,0:T(8,128)(2,1)} %copy.112), calls=%async_computation.3 | async-start | bytes 4194304 | tf_op jit(solution)/shard_map/all_to_all | solution.py:39
  267.4 3.0 copy.114
  270.4 23.2 %all-to-all-done.3 = bf16[128,32,256]{2,1,0:T(8,128)(2,1)} async-done(((bf16[128,32,256]{2,1,0:T(8,128)(2,1)}), bf16[128,32,256]{2,1,0:T(8,128)(2,1)}, u32[]{:S(2)}, u32[]{:S(2)}) %all-to-all-start.3) | async-done | bytes 2097184 | tf_op jit(solution)/shard_map/all_to_all | solution.py:39
  293.6 5.7 %all-to-all-start.4 = ((bf16[128,32,256]{2,1,0:T(8,128)(2,1)}), bf16[128,32,256]{2,1,0:T(8,128)(2,1)}, u32[]{:S(2)}, u32[]{:S(2)}) async-start(bf16[128,32,256]{2,1,0:T(8,128)(2,1)} %copy.114), calls=%async_computation.4 | async-start | bytes 4194304 | tf_op jit(solution)/shard_map/all_to_all | solution.py:40
  299.3 1.8 copy.113
  301.2 24.2 %all-to-all-done.4 = bf16[128,32,256]{2,1,0:T(8,128)(2,1)} async-done(((bf16[128,32,256]{2,1,0:T(8,128)(2,1)}), bf16[128,32,256]{2,1,0:T(8,128)(2,1)}, u32[]{:S(2)}, u32[]{:S(2)}) %all-to-all-start.4) | async-done | bytes 2097184 | tf_op jit(solution)/shard_map/all_to_all | solution.py:40
  325.4 1.8 copy.115
  327.2 0.8 convolution_convert_fusion
  328.0 2.5 copy.117
  330.5 4.6 %all-to-all-start.5 = ((bf16[16,256,256]{2,0,1:T(8,128)(2,1)}), bf16[16,256,256]{2,0,1:T(8,128)(2,1)S(1)}, u32[]{:S(2)}, u32[]{:S(2)}) async-start(bf16[16,256,256]{2,0,1:T(8,128)(2,1)} %copy.117), calls=%async_computation.5 | async-start | bytes 4194304 | tf_op jit(solution)/shard_map/all_to_all | solution.py:43
  335.4 5.1 %fusion.59 = f32[32,256,128]{1,2,0:T(8,128)} fusion(bf16[2,128,128]{2,1,0:T(8,128)(2,1)S(1)} %copy-done.11, f32[32,256,128]{1,2,0:T(8,128)} %copy-done.5, f32[128]{0:T(128)S(1)} %get-tuple-element.16, f32[128]{0:T(128)S(1)} %get-tuple-element.13, f32[32,256]{1,0:T(8,128)S(1)} %add_rsqrt_fusion.2, f32[32,256]{1,0:T(8,128)S(1)} %broadcast_multiply_fusion.2), kind=kOutput, calls=%fused_computation.84 | convolution fusion | flops 273678336 | bytes 8487936 | tf_op jit(solution)/shard_map/rnz,zy->rny/dot_general | solution.py:45
  340.5 20.7 %all-to-all-done.5 = bf16[16,256,256]{2,0,1:T(8,128)(2,1)S(1)} async-done(((bf16[16,256,256]{2,0,1:T(8,128)(2,1)}), bf16[16,256,256]{2,0,1:T(8,128)(2,1)S(1)}, u32[]{:S(2)}, u32[]{:S(2)}) %all-to-all-start.5) | async-done | bytes 2097184 | tf_op jit(solution)/shard_map/all_to_all | solution.py:43
  362.9 1.1 fusion.37
  364.2 0.9 copy-done.6
  365.1 1.3 copy-done.9
  366.4 4.2 %multiply_add_fusion = f32[32,256,128]{1,2,0:T(8,128)} fusion(f32[32,256,128]{1,2,0:T(8,128)S(1)} %copy-done.6, f32[32,256,128]{1,2,0:T(8,128)S(1)} %copy-done.9, bf16[128,32,256]{2,1,0:T(8,128)(2,1)S(1)} %bitcast.133, bf16[2,128,128]{2,1,0:T(8,128)(2,1)S(1)} %copy-done.17), kind=kOutput, calls=%fused_computation.61 | convolution fusion | flops 273678336 | bytes 14712832 | tf_op jit(solution)/shard_map/crn,cz->rnz/dot_general | solution.py:46
  370.5 5.6 %copy.124 = f32[32,256,128]{2,1,0:T(8,128)} copy(f32[32,256,128]{1,2,0:T(8,128)} %multiply_add_fusion) | data formatting | bytes 8388608 | tf_op jit(solution)/shard_map/add | solution.py:47
  (66 shorter events, 6.4 us)
Async XLA Ops:
  6.5 124.7 %copy-start = (bf16[1024,128]{1,0:T(8,128)(2,1)S(1)}, bf16[1024,128]{1,0:T(8,128)(2,1)}, u32[]{:S(2)}) copy-start(bf16[1024,128]{1,0:T(8,128)(2,1)} %param.17) | copy-start | bytes 786436
  6.6 88.8 %all-gather.2.cloned.1.call-start = ((), (), s32[]{:S(2)}) async-start(), calls=%async_computation.6 | async-start | bytes 9437184 | tf_op jit(solution)/shard_map/all_gather | solution.py:25
  6.6 5.8 %copy-start.4 = (bf16[512,32,256]{2,1,0:T(8,128)(2,1)S(1)}, bf16[512,32,256]{2,1,0:T(8,128)(2,1)}, u32[]{:S(2)}) copy-start(bf16[512,32,256]{2,1,0:T(8,128)(2,1)} %param.14) | copy-start | bytes 25165828
  12.4 14.0 %copy-start.14 = (f32[2,256]{1,0:T(2,128)S(1)}, f32[2,256]{1,0:T(2,128)}, u32[]{:S(2)}) copy-start(f32[2,256]{1,0:T(2,128)} %param.15) | copy-start | bytes 6148
  26.4 7.3 %copy-start.18 = (bf16[256,64]{0,1:T(8,128)(2,1)S(1)}, bf16[256,64]{0,1:T(8,128)(2,1)}, u32[]{:S(2)}) copy-start(bf16[256,64]{0,1:T(8,128)(2,1)} %param.16) | copy-start | bytes 98308
  44.2 6.2 %copy-start.12 = (s32[32,256]{1,0:T(8,128)S(1)}, s32[32,256]{1,0:T(8,128)}, u32[]{:S(2)}) copy-start(s32[32,256]{1,0:T(8,128)} %param.13) | copy-start | bytes 98308
  44.2 6.2 %copy-start.15 = (f32[2,2,128]{2,1,0:T(2,128)S(1)}, f32[2,2,128]{2,1,0:T(2,128)}, u32[]{:S(2)}) copy-start(f32[2,2,128]{2,1,0:T(2,128)} %param.19) | copy-start | bytes 6148
  115.0 16.2 %copy-start.7 = (f32[32,256,128]{1,2,0:T(8,128)S(1)}, f32[32,256,128]{1,2,0:T(8,128)}, u32[]{:S(2)}) copy-start(f32[32,256,128]{1,2,0:T(8,128)} %copy.98) | copy-start | bytes 12582916
  115.0 16.2 %copy-start.13 = (f32[128]{0:T(128)S(1)}, f32[128]{0:T(128)}, u32[]{:S(2)}) copy-start(f32[128]{0:T(128)} %param.18) | copy-start | bytes 1540
  134.4 3.7 copy-start.2
  134.4 1.1 copy-start.10
  146.2 30.7 %all-to-all-start = ((bf16[128,32,256]{2,1,0:T(8,128)(2,1)}), bf16[128,32,256]{2,1,0:T(8,128)(2,1)}, u32[]{:S(2)}, u32[]{:S(2)}) async-start(bf16[128,32,256]{2,1,0:T(8,128)(2,1)} %copy.102), calls=%async_computation | async-start | bytes 4194304 | tf_op jit(solution)/shard_map/all_to_all | solution.py:39
  176.9 31.5 %all-to-all-start.1 = ((bf16[128,32,256]{2,1,0:T(8,128)(2,1)}), bf16[128,32,256]{2,1,0:T(8,128)(2,1)}, u32[]{:S(2)}, u32[]{:S(2)}) async-start(bf16[128,32,256]{2,1,0:T(8,128)(2,1)} %copy.104), calls=%async_computation.1 | async-start | bytes 4194304 | tf_op jit(solution)/shard_map/all_to_all | solution.py:40
  211.0 7.5 %copy-start.16 = (f32[2,2,128]{2,1,0:T(2,128)S(1)}, f32[2,2,128]{2,1,0:T(2,128)}, u32[]{:S(2)}) copy-start(f32[2,2,128]{2,1,0:T(2,128)} %param.22) | copy-start | bytes 6148
  211.0 7.7 %copy-start.11 = (bf16[2,128,128]{2,1,0:T(8,128)(2,1)S(1)}, bf16[2,128,128]{2,1,0:T(8,128)(2,1)}, u32[]{:S(2)}) copy-start(bf16[2,128,128]{2,1,0:T(8,128)(2,1)} %param.21) | copy-start | bytes 196612
  213.5 30.9 %all-to-all-start.2 = ((bf16[16,256,256]{2,0,1:T(8,128)(2,1)}), bf16[16,256,256]{2,0,1:T(8,128)(2,1)S(1)}, u32[]{:S(2)}, u32[]{:S(2)}) async-start(bf16[16,256,256]{2,0,1:T(8,128)(2,1)} %copy.106), calls=%async_computation.2 | async-start | bytes 4194304 | tf_op jit(solution)/shard_map/all_to_all | solution.py:43
  245.4 2.2 copy-start.3
  245.4 3.5 copy-start.8
  245.4 3.5 copy-start.17
  250.5 3.4 copy-start.5
  262.0 31.6 %all-to-all-start.3 = ((bf16[128,32,256]{2,1,0:T(8,128)(2,1)}), bf16[128,32,256]{2,1,0:T(8,128)(2,1)}, u32[]{:S(2)}, u32[]{:S(2)}) async-start(bf16[128,32,256]{2,1,0:T(8,128)(2,1)} %copy.112), calls=%async_computation.3 | async-start | bytes 4194304 | tf_op jit(solution)/shard_map/all_to_all | solution.py:39
  293.6 31.8 %all-to-all-start.4 = ((bf16[128,32,256]{2,1,0:T(8,128)(2,1)}), bf16[128,32,256]{2,1,0:T(8,128)(2,1)}, u32[]{:S(2)}, u32[]{:S(2)}) async-start(bf16[128,32,256]{2,1,0:T(8,128)(2,1)} %copy.114), calls=%async_computation.4 | async-start | bytes 4194304 | tf_op jit(solution)/shard_map/all_to_all | solution.py:40
  330.5 30.7 %all-to-all-start.5 = ((bf16[16,256,256]{2,0,1:T(8,128)(2,1)}), bf16[16,256,256]{2,0,1:T(8,128)(2,1)S(1)}, u32[]{:S(2)}, u32[]{:S(2)}) async-start(bf16[16,256,256]{2,0,1:T(8,128)(2,1)} %copy.117), calls=%async_computation.5 | async-start | bytes 4194304 | tf_op jit(solution)/shard_map/all_to_all | solution.py:43
  362.9 2.2 copy-start.6
  362.9 3.5 copy-start.9
  366.4 9.7 %copy-start.1 = (bf16[1024,128]{1,0:T(8,128)(2,1)S(1)}, bf16[1024,128]{1,0:T(8,128)(2,1)}, u32[]{:S(2)}) copy-start(bf16[1024,128]{1,0:T(8,128)(2,1)} %param.17) | copy-start | bytes 786436
Sparse Core Ops, SparseCore 0:
  44.3 50.9 all-gather.1
where the time goes:
time: 387 us; the launch traced here: 383 us
  waiting for transfers between devices  181 us (47%)
  local copies, waits for them, and re-layouts  63.1 us (16%)
  matrix products  54.9 us (14%)
  other arithmetic  39.3 us (10%)
  starting transfers between devices  30.5 us (8%)
  between operations  14.1 us (4%)
    all_to_all x2, waiting for transfers between devices, triangle_update(): right_chan = lax.all_to_all(right_act, 'dap', 0, 1, tiled=True)  48.6 us
    all_to_all x2, waiting for transfers between devices, triangle_update(): left_chan = lax.all_to_all(left_act, 'dap', 0, 1, tiled=True)  46.3 us
    all_gather x1, waiting for transfers between devices, outer_product_mean(): lax.all_gather(proj_all[:, :, opm_dim:], 'dap', axis=1, tiled=True)  44.9 us
    all_to_all x2, waiting for transfers between devices, triangle_update(): mixed_rows = lax.all_to_all(mixed_chan, 'dap', 1, 0, tiled=True)  41.5 us
    dot_general x1, matrix products, outer_product_mean(): jnp.einsum('sip,sjq->ijpq', proj_all[:, :, :opm_dim], right_full, preferr...  19.7 us
    reduce_sum x5, other arithmetic, norm_over(): chan_var = jnp.mean(centered * centered, axis=norm_axis, keepdims=True)  16.5 us
    convert_element_type x1, local copies, waits for them, and re-layouts, outer_product_mean(): outer_prod.astype(jnp.bfloat16)  16.2 us
    convert_element_type x4, local copies, waits for them, and re-layouts, gated_act(): (mask_f * jax.nn.sigmoid(proj_vals[tri_dim:]) * proj_vals[:tri_dim]).asty...  15.2 us
  transfers between devices with their start and end apart: 7, of which 7 were waited for; matrix products, arithmetic and copies ran while one was open for 7% of the time, Pallas kernels for 0%

commit v1 on v0

v1 whole, which is shorter than its diff:
```python
import functools

import jax
import jax.numpy as jnp
from jax import lax
from jax.experimental import pallas as pl
from jax.experimental.pallas import tpu as pltpu
from jax.sharding import PartitionSpec as P

LN_EPS = 1e-5
LANES = 128
MESH = pl.DeviceIdType.MESH


def norm_over(values, norm_scale, norm_shift, norm_axis):
    chan_mean = jnp.mean(values, axis=norm_axis, keepdims=True)
    centered = values - chan_mean
    chan_var = jnp.mean(centered * centered, axis=norm_axis, keepdims=True)
    return (centered * lax.rsqrt(chan_var + LN_EPS) * norm_scale + norm_shift).astype(jnp.bfloat16)


def outer_product_mean(value_a7, opm_norm, opm_proj, opm_out, opm_bias):
    value_a9 = value_a7.shape[0]
    opm_dim = opm_proj.shape[1] // 2
    value_a8 = norm_over(value_a7.astype(jnp.float32), opm_norm[0], opm_norm[1], -1)
    proj_all = jnp.einsum("srm,mp->srp", value_a8, opm_proj, preferred_element_type=jnp.float32).astype(jnp.bfloat16)
    right_full = lax.all_gather(proj_all[:, :, opm_dim:], "dap", axis=1, tiled=True)
    outer_prod = jnp.einsum("sip,sjq->ijpq", proj_all[:, :, :opm_dim], right_full, preferred_element_type=jnp.float32) / value_a9
    local_rows = outer_prod.shape[0]
    residues = outer_prod.shape[1]
    outer_flat = outer_prod.astype(jnp.bfloat16).reshape(local_rows, residues, opm_dim * opm_dim)
    return jnp.einsum("ijf,fz->ijz", outer_flat, opm_out, preferred_element_type=jnp.float32) + opm_bias


def _col(v, n):
    return jnp.broadcast_to(v.astype(jnp.float32)[:, None], (v.shape[0], n))


def _norm_rows(v, scale, shift):
    mean = jnp.mean(v, axis=0, keepdims=True)
    cen = v - mean
    var = jnp.mean(cen * cen, axis=0, keepdims=True)
    return (cen * lax.rsqrt(var + LN_EPS) * scale + shift).astype(jnp.bfloat16)


def _entry_barrier(me, n):
    barrier = pltpu.get_barrier_semaphore()
    for s in range(1, n):
        pl.semaphore_signal(barrier, inc=1, device_id={"dap": lax.rem(me + s, n)}, device_id_type=MESH)
    pl.semaphore_wait(barrier, n - 1)


def _tri_kernel(n, incoming, z_hbm, mask_ref, w_ref, wout_ref, nrm_ref, o_hbm,
                zb, gb, st, snd, ra, rb, xs, xr, tb, ob, zsem, osem, ss_ab, rs_ab, ss_x, rs_x):
    me = lax.axis_index("dap")
    rows, chan, cols = zb.shape
    ch_rows = snd.shape[3]
    chunks = rows // ch_rows
    cown = chan // n
    halves = cols // LANES
    pst = st.shape[2] // ch_rows
    pxt = tb.shape[1] // chan
    slot = ch_rows

    def zcopy(ch):
        at = pl.ds(ch * ch_rows, ch_rows)
        return pltpu.make_async_copy(z_hbm.at[at], zb.at[at], zsem.at[ch])

    def ab_copy(t, ch, src, dst):
        buf = rb if t else ra
        return pltpu.make_async_remote_copy(
            src_ref=snd.at[t, ch, pl.ds(pl.multiple_of(dst * cown, cown), cown)],
            dst_ref=buf.at[src, :, pl.ds(ch * slot, slot)],
            send_sem=ss_ab.at[t, ch, dst], recv_sem=rs_ab.at[t, ch, src],
            device_id={"dap": dst}, device_id_type=MESH)

    def x_copy(ch, src, dst):
        return pltpu.make_async_remote_copy(
            src_ref=xs.at[ch, dst], dst_ref=xr.at[ch, pl.ds(pl.multiple_of(src * cown, cown), cown)],
            send_sem=ss_x.at[ch, dst], recv_sem=rs_x.at[ch, src],
            device_id={"dap": dst}, device_id_type=MESH)

    for ch in range(chunks):
        zcopy(ch).start()
    _entry_barrier(me, n)

    scale, shift = nrm_ref[0], nrm_ref[1]
    xscale, xshift = nrm_ref[2], nrm_ref[3]

    for ch in range(chunks):
        zcopy(ch).wait()

        @pl.loop(0, ch_rows)
        def _(i, ch=ch):
            r = ch * ch_rows + i
            y = _norm_rows(zb[r], scale, shift)
            q = jnp.dot(w_ref[...], y, preferred_element_type=jnp.float32)
            m = mask_ref[pl.ds(r, 1), :]
            a = m * jax.nn.sigmoid(q[chan:2 * chan]) * q[:chan]
            b = m * jax.nn.sigmoid(q[3 * chan:4 * chan]) * q[2 * chan:3 * chan]
            gb[r] = jax.nn.sigmoid(q[4 * chan:])
            at = pl.ds(pl.multiple_of(i * pst, 8), chan)
            for h in range(halves):
                st[0, h, at, :] = a[:, h * LANES:(h + 1) * LANES]
                st[1, h, at, :] = b[:, h * LANES:(h + 1) * LANES]

        @pl.loop(0, chan, unroll=8)
        def _(c, ch=ch):
            for t in range(2):
                for h in range(halves):
                    snd[t, ch, c, :, h * LANES:(h + 1) * LANES] = st[t, h, pl.ds(c, ch_rows, stride=pst), :].astype(jnp.bfloat16)

        own = pl.ds(pl.multiple_of(me * cown, cown), cown)
        if incoming:
            order = ((1, ch), (0, ch))
        else:
            order = ((1, ch),) if ch < chunks - 1 else ((1, ch),) + tuple((0, k) for k in range(chunks))
        for t, k in order:
            for s in range(1, n):
                ab_copy(t, k, me, lax.rem(me + s, n)).start()
        ra[me, :, ch * slot:(ch + 1) * slot] = snd[0, ch, own]
        rb[me, :, ch * slot:(ch + 1) * slot] = snd[1, ch, own]

    def wait_ab(t, ch):
        for s in range(1, n):
            ab_copy(t, ch, lax.rem(me + s, n), me).wait_recv()

    def send_x(ch):
        for s in range(1, n):
            x_copy(ch, me, lax.rem(me + s, n)).start()
        xr[ch, pl.ds(pl.multiple_of(me * cown, cown), cown)] = xs[ch, me]

    for ch in range(chunks):
        wait_ab(1, ch)
    if incoming:
        for ch in range(chunks):
            wait_ab(0, ch)

        @pl.loop(0, cown)
        def _(c):
            x = lax.dot_general(ra[:, c].reshape(n * rows, cols), rb[:, c].reshape(n * rows, cols),
                                (((0,), (0,)), ((), ())), preferred_element_type=jnp.float32)
            x = x.astype(jnp.bfloat16).reshape(n, chunks, ch_rows, cols)
            for ch in range(chunks):
                xs[ch, :, c] = x[:, ch]
        for ch in range(chunks):
            send_x(ch)
    else:
        for ch in range(chunks):
            wait_ab(0, ch)

            @pl.loop(0, cown)
            def _(c, ch=ch):
                x = lax.dot_general(ra[:, c, ch * slot:(ch + 1) * slot].reshape(n * ch_rows, cols),
                                    rb[:, c].reshape(n * rows, cols),
                                    (((1,), (1,)), ((), ())), preferred_element_type=jnp.float32)
                xs[ch, :, c] = x.astype(jnp.bfloat16).reshape(n, ch_rows, cols)
            send_x(ch)

    for ch in range(chunks):
        for s in range(1, n):
            x_copy(ch, lax.rem(me + s, n), me).wait_recv()

        @pl.loop(0, chan, unroll=8)
        def _(c, ch=ch):
            at = pl.ds(pl.multiple_of(c * pxt, 8), ch_rows)
            for h in range(halves):
                tb[h, at, :] = xr[ch, c, :, h * LANES:(h + 1) * LANES].astype(jnp.float32)

        @pl.loop(0, ch_rows)
        def _(i, ch=ch):
            r = ch * ch_rows + i
            x = jnp.concatenate([tb[h, pl.ds(i, chan, stride=pxt), :] for h in range(halves)], axis=1)
            xn = _norm_rows(x, xscale, xshift)
            upd = jnp.dot(wout_ref[...], xn, preferred_element_type=jnp.float32)
            ob[r] = zb[r] + gb[r] * upd
        at = pl.ds(ch * ch_rows, ch_rows)
        pltpu.make_async_copy(ob.at[at], o_hbm.at[at], osem.at[ch]).start()

    for ch in range(chunks):
        at = pl.ds(ch * ch_rows, ch_rows)
        pltpu.make_async_copy(ob.at[at], o_hbm.at[at], osem.at[ch]).wait()
        for s in range(1, n):
            dst = lax.rem(me + s, n)
            ab_copy(0, ch, me, dst).wait_send()
            ab_copy(1, ch, me, dst).wait_send()
            x_copy(ch, me, dst).wait_send()


def _tri_call(n, incoming, z_cm, mask_f, w_proj, w_gate, norm_pair, norm_mix, w_out):
    rows, chan, cols = z_cm.shape
    cown = chan // n
    chunks = 2
    ch_rows = rows // chunks
    halves = cols // LANES
    w_all = jnp.concatenate([w_proj, w_gate], axis=1).T
    nrm = jnp.stack([_col(norm_pair[0], cols), _col(norm_pair[1], cols), _col(norm_mix[0], cols), _col(norm_mix[1], cols)])
    vm = pl.BlockSpec(memory_space=pltpu.VMEM)
    hbm = pl.BlockSpec(memory_space=pl.ANY)
    return pl.pallas_call(
        functools.partial(_tri_kernel, n, incoming),
        out_shape=jax.ShapeDtypeStruct(z_cm.shape, jnp.float32),
        in_specs=[hbm, vm, vm, vm, vm],
        out_specs=hbm,
        scratch_shapes=[
            pltpu.VMEM((rows, chan, cols), jnp.float32),
            pltpu.VMEM((rows, chan, cols), jnp.float32),
            pltpu.VMEM((2, halves, ch_rows * (chan + 8), LANES), jnp.float32),
            pltpu.VMEM((2, chunks, chan, ch_rows, cols), jnp.bfloat16),
            pltpu.VMEM((n, cown, rows, cols), jnp.bfloat16),
            pltpu.VMEM((n, cown, rows, cols), jnp.bfloat16),
            pltpu.VMEM((chunks, n, cown, ch_rows, cols), jnp.bfloat16),
            pltpu.VMEM((chunks, chan, ch_rows, cols), jnp.bfloat16),
            pltpu.VMEM((halves, chan * (ch_rows + 8), LANES), jnp.float32),
            pltpu.VMEM((rows, chan, cols), jnp.float32),
            pltpu.SemaphoreType.DMA((chunks,)),
            pltpu.SemaphoreType.DMA((chunks,)),
            pltpu.SemaphoreType.DMA((2, chunks, n)),
            pltpu.SemaphoreType.DMA((2, chunks, n)),
            pltpu.SemaphoreType.DMA((chunks, n)),
            pltpu.SemaphoreType.DMA((chunks, n)),
        ],
        compiler_params=pltpu.CompilerParams(collective_id=2 if incoming else 1, has_side_effects=True, vmem_limit_bytes=60 * 1024 * 1024),
        name="tri_in" if incoming else "tri_out",
    )(z_cm, mask_f, w_all, w_out.T, nrm)


def solution(mesh):
    row_spec = P(("data", "dap"), None, None)
    mask_spec = P(("data", "dap"), None)
    array_b8 = P(None, ("data", "dap"), None)
    replicated = P()

    def local_program(pair_loc, mask_loc, value_a7, opm_norm, opm_proj, opm_out, opm_bias, tri_norm, tri_proj, tri_gate, tri_xnorm, tri_out):
        n = lax.axis_size("dap")
        mask_f = mask_loc.astype(jnp.float32)
        pair_zero = pair_loc + outer_product_mean(value_a7, opm_norm, opm_proj, opm_out, opm_bias)
        z = jnp.swapaxes(pair_zero, 1, 2)
        for t in range(2):
            z = _tri_call(n, t == 1, z, mask_f, tri_proj[t], tri_gate[t], tri_norm[t], tri_xnorm[t], tri_out[t])
        return jnp.swapaxes(z, 1, 2)

    return jax.shard_map(local_program, mesh=mesh, in_specs=(row_spec, mask_spec, array_b8) + (replicated,) * 9, out_specs=row_spec, check_vma=False)
```

time: 387 us -> 324 us (0.84)
  Pallas kernels: 0 us -> 175 us
  waiting for transfers between devices: 181 us -> 39 us
  local copies, waits for them, and re-layouts: 63.1 us -> 31.3 us
  starting transfers between devices: 30.5 us -> 0.01 us
  matrix products: 54.9 us -> 34 us
  other arithmetic: 39.3 us -> 30.7 us
    pallas_call x0 -> x2, Pallas kernels: none -> 175 us  [_tri_call(): pl.pallas_call(functools.partial(_tri_kernel, n, incoming), out_shape=jax...]
    all_to_all x6 -> x0, waiting for transfers between devices: 136 us -> none  [the longest x2 48.6 us: triangle_update(): right_chan = lax.all_to_all(right_act, 'dap', 0, 1, tiled=True)]
    all_to_all x6 -> x0, starting transfers between devices: 30.5 us -> none  [the longest x2 11.1 us: triangle_update(): right_chan = lax.all_to_all(right_act, 'dap', 0, 1, tiled=True)]
    dot_general x8 -> x0, matrix products: 22.6 us -> none  [the longest x2 10.1 us: triangle_update(): jnp.einsum('rnz,zy->rny', pair_norm, w_gate, preferred_element_type=jnp.f...]
    convert_element_type x8 -> x0, local copies, waits for them, and re-layouts: 20.7 us -> none  [the longest x4 15.2 us: gated_act(): (mask_f * jax.nn.sigmoid(proj_vals[tri_dim:]) * proj_vals[:tri_dim]).asty...]
    all_to_all x5 -> x0, local copies, waits for them, and re-layouts: 8 us -> none  [the longest x2 3.65 us: triangle_update(): left_chan = lax.all_to_all(left_act, 'dap', 0, 1, tiled=True)]
    convert_element_type x3 -> x1, other arithmetic: 6.91 us -> 0.6 us  [local_program(): mask_f = mask_loc.astype(jnp.float32)]
    all_gather x1, waiting for transfers between devices: 44.9 us -> 38.9 us  [outer_product_mean(): lax.all_gather(proj_all[:, :, opm_dim:], 'dap', axis=1, tiled=True)]
  transfers between devices with their start and end apart: 7 -> 1, of which waited for: 7 -> 1; matrix products, arithmetic and copies ran while one was open for 7% -> 4% of each run, Pallas kernels for 0% -> 0%
where the time goes in v1:
time: 324 us; the launch traced here: 323 us
  Pallas kernels  175 us (54%)
  waiting for transfers between devices  39 us (12%)
  matrix products  34 us (10%)
  local copies, waits for them, and re-layouts  31.3 us (10%)
  other arithmetic  30.7 us (9%)
  between operations  13.7 us (4%)
    pallas_call x2, Pallas kernels, _tri_call(): pl.pallas_call(functools.partial(_tri_kernel, n, incoming), out_shape=jax...  175 us
    all_gather x1, waiting for transfers between devices, outer_product_mean(): lax.all_gather(proj_all[:, :, opm_dim:], 'dap', axis=1, tiled=True)  38.9 us
    dot_general x1, matrix products, outer_product_mean(): jnp.einsum('sip,sjq->ijpq', proj_all[:, :, :opm_dim], right_full, preferr...  19.6 us
    convert_element_type x1, local copies, waits for them, and re-layouts, outer_product_mean(): outer_prod.astype(jnp.bfloat16)  16.3 us
    reduce_sum x1, other arithmetic, norm_over(): chan_var = jnp.mean(centered * centered, axis=norm_axis, keepdims=True)  13.8 us
    dot_general x1, matrix products, outer_product_mean(): jnp.einsum('srm,mp->srp', value_a8, opm_proj, preferred_element_type=jnp....  9.32 us
    unnamed x31, local copies, waits for them, and re-layouts  7.78 us
    convert_element_type x1, other arithmetic, norm_over(): (centered * lax.rsqrt(chan_var + LN_EPS) * norm_scale + norm_shift).astyp...  7.29 us
  transfers between devices with their start and end apart: 1, of which 1 were waited for; matrix products, arithmetic and copies ran while one was open for 4% of the time, Pallas kernels for 0%

profile of v1, /device:TPU:81, one launch (start us, length us, event | category | flops | bytes accessed | tf_op | source)
XLA Modules:
  0.0 323.3 jit_solution(3304063783096555753)
XLA Ops:
  6.5 0.0 copy-start
  6.6 0.0 all-gather.2.cloned.1.call-start
  6.6 5.8 %convert_reduce_fusion = f32[512,32]{1,0:T(8,128)S(1)} fusion(bf16[512,32,256]{2,1,0:T(8,128)(2,1)} %param.14), kind=kLoop, calls=%fused_computation.2 | loop fusion | flops 8372224 | bytes 8454144 | tf_op jit(solution)/shard_map/reduce_sum | solution.py:16
  12.4 0.0 copy-done.1
  12.4 13.8 %fusion.2 = f32[512,32]{1,0:T(8,128)S(1)} fusion(bf16[512,32,256]{2,1,0:T(8,128)(2,1)S(1)} %copy-done.1, f32[512,32]{1,0:T(8,128)S(1)} %broadcast_multiply_fusion), kind=kLoop, calls=%fused_computation.5 | loop fusion | flops 16760832 | bytes 8519680 | tf_op jit(solution)/shard_map/reduce_sum | solution.py:18
  26.3 0.0 copy-done.8
  26.3 0.0 copy-start.11
  26.3 7.3 %fusion.5 = bf16[512,32,256]{2,1,0:T(8,128)(2,1)S(1)} fusion(bf16[512,32,256]{2,1,0:T(8,128)(2,1)S(1)} %copy-done.1, f32[256]{0:T(256)S(1)} %bitcast.58, f32[256]{0:T(256)S(1)} %bitcast.57, f32[512,32]{1,0:T(8,128)S(1)} %add_rsqrt_fusion, f32[512,32]{1,0:T(8,128)S(1)} %broadcast_multiply_fusion), kind=kLoop, calls=%fused_computation.8 | loop fusion | flops 25165824 | bytes 16910336 | tf_op jit(solution)/shard_map/convert_element_type | solution.py:19
  33.6 0.0 copy-done.11
  33.6 9.3 %fusion.10 = bf16[512,32,64]{0,2,1:T(8,128)(2,1)S(1)} fusion(bf16[512,32,256]{2,1,0:T(8,128)(2,1)S(1)} %fusion.5, bf16[256,64]{0,1:T(8,128)(2,1)S(1)} %copy-done.11), kind=kOutput, calls=%fused_computation.14 | convolution fusion | flops 537919488 | bytes 10518528 | tf_op jit(solution)/shard_map/srm,mp->srp/dot_general | solution.py:26
  43.0 0.0 copy-start.3
  43.0 0.0 copy-start.4
  43.0 0.0 copy-start.5
  43.0 0.0 copy-start.6
  43.0 0.0 copy-start.9
  43.0 0.0 copy-start.10
  43.0 1.1 slice.92
  44.1 0.1 all-gather.2.cloned.1.call-update
  44.1 5.8 %copy.42 = f32[32,256,128]{1,2,0:T(8,128)} copy(f32[32,256,128]{2,1,0:T(8,128)} %param.12) | data formatting | bytes 8388608 | tf_op args[0]
  50.0 0.0 copy-done.3
  50.0 0.1 copy.55
  50.1 0.0 copy-done.4
  50.1 0.1 copy.56
  50.3 0.0 copy-done.5
  50.3 0.7 copy.57
  51.0 0.6 convert_element_type.23.mask_ref
  51.6 0.1 copy.58
  51.7 0.1 copy.59
  51.8 0.7 copy.60
  52.6 0.7 maximum_bitcast_fusion.w_ref
  53.2 0.7 maximum_bitcast_fusion.1.w_ref
  53.9 0.1 stack_broadcast_in_dim.57
  54.0 0.1 stack_broadcast_in_dim.59
  54.1 0.1 stack_broadcast_in_dim.61
  54.2 0.1 stack_broadcast_in_dim.63
  54.3 0.9 pad_maximum_fusion.nrm_ref
  55.1 0.1 stack_broadcast_in_dim.65
  55.2 0.1 stack_broadcast_in_dim.67
  55.3 0.1 stack_broadcast_in_dim.69
  55.4 0.1 stack_broadcast_in_dim.71
  55.5 0.9 pad_maximum_fusion.1.nrm_ref
  56.3 38.9 %all-gather.2.cloned.1.call-done = bf16[512,256,32]{0,2,1:T(8,128)(2,1)} async-done(((bf16[512,32,32]{0,2,1:T(8,128)(2,1)}), bf16[512,256,32]{0,2,1:T(8,128)(2,1)}) %all-gather.2.cloned.1.call-update) | async-done | bytes 8388624 | tf_op jit(solution)/shard_map/all_gather | solution.py:27
  95.3 19.6 %fusion.6 = bf16[32,256,32,32]{1,2,0,3:T(8,128)(2,1)} fusion(bf16[512,256,32,1]{0,2,1,3:T(8,128)(2,1)} %bitcast.59, bf16[512,32,64]{0,2,1:T(8,128)(2,1)S(1)} %fusion.10), kind=kOutput, calls=%fused_computation.9 | convolution fusion | flops 8606711808 | bytes 26214400 | tf_op jit(solution)/shard_map/sip,sjq->ijpq/dot_general | solution.py:28
  114.9 16.3 %copy.39 = bf16[32,256,32,32]{1,3,2,0:T(8,128)(2,1)S(1)} copy(bf16[32,256,32,32]{1,2,0,3:T(8,128)(2,1)} %fusion.6) | data formatting | bytes 33554432 | tf_op jit(solution)/shard_map/convert_element_type | solution.py:31
  131.2 5.1 %add_bitcast_fusion.z_hbm = f32[32,128,256]{2,1,0:T(8,128)} fusion(f32[32,256,128]{1,2,0:T(8,128)S(1)} %copy-done.2, f32[128]{0:T(128)S(1)} %copy-done.7, bf16[32,256,1024]{1,2,0:T(8,128)(2,1)S(1)} %bitcast.49, bf16[1024,128]{1,0:T(8,128)(2,1)S(1)} %copy-done), kind=kOutput, calls=%fused_computation.13 | convolution fusion | flops 2149580800 | bytes 25428480 | tf_op jit(solution)/shard_map/ijf,fz->ijz/dot_general | solution.py:32
  136.2 85.1 %tri_out.1.z_hbm = f32[32,128,256]{2,1,0:T(8,128)} custom-call(f32[32,128,256]{2,1,0:T(8,128)} %add_bitcast_fusion.z_hbm, f32[32,256]{1,0:T(8,128)} %convert_element_type.23.mask_ref, bf16[640,128]{1,0:T(8,128)(2,1)} %maximum_bitcast_fusion.w_ref, bf16[128,128]{1,0:T(8,128)(2,1)} %bitcast.53, f32[4,128,256]{2,1,0:T(8,128)} %pad_maximum_fusion.nrm_ref), custom_call_target="tpu_custom_call" | custom-call | tf_op jit(solution)/shard_map/tri_out/pallas_call | solution.py:200
  221.3 89.5 %tri_in.1 = f32[32,128,256]{2,1,0:T(8,128)} custom-call(f32[32,128,256]{2,1,0:T(8,128)} %tri_out.1.z_hbm, f32[32,256]{1,0:T(8,128)} %convert_element_type.23.mask_ref, bf16[640,128]{1,0:T(8,128)(2,1)} %maximum_bitcast_fusion.1.w_ref, bf16[128,128]{1,0:T(8,128)(2,1)} %bitcast.54, f32[4,128,256]{2,1,0:T(8,128)} %pad_maximum_fusion.1.nrm_ref), custom_call_target="tpu_custom_call" | custom-call | tf_op jit(solution)/shard_map/tri_in/pallas_call | solution.py:200
  310.9 5.6 %copy.49 = f32[32,256,128]{2,1,0:T(8,128)} copy(f32[32,256,128]{1,2,0:T(8,128)} %bitcast.50) | data formatting | bytes 8388608 | tf_op jit(solution)/shard_map/transpose | solution.py:241
  (18 shorter events, 0.1 us)
Async XLA Ops:
  6.5 124.6 %copy-start = (bf16[1024,128]{1,0:T(8,128)(2,1)S(1)}, bf16[1024,128]{1,0:T(8,128)(2,1)}, u32[]{:S(2)}) copy-start(bf16[1024,128]{1,0:T(8,128)(2,1)} %param.17) | copy-start | bytes 786436
  6.6 19.7 %copy-start.8 = (f32[2,256]{1,0:T(2,128)S(1)}, f32[2,256]{1,0:T(2,128)}, u32[]{:S(2)}) copy-start(f32[2,256]{1,0:T(2,128)} %param.15) | copy-start | bytes 6148
  6.6 88.7 %all-gather.2.cloned.1.call-start = ((), (), s32[]{:S(2)}) async-start(), calls=%async_computation | async-start | bytes 9437184 | tf_op jit(solution)/shard_map/all_gather | solution.py:27
  6.6 5.8 %copy-start.1 = (bf16[512,32,256]{2,1,0:T(8,128)(2,1)S(1)}, bf16[512,32,256]{2,1,0:T(8,128)(2,1)}, u32[]{:S(2)}) copy-start(bf16[512,32,256]{2,1,0:T(8,128)(2,1)} %param.14) | copy-start | bytes 25165828
  26.3 7.3 %copy-start.11 = (bf16[256,64]{0,1:T(8,128)(2,1)S(1)}, bf16[256,64]{0,1:T(8,128)(2,1)}, u32[]{:S(2)}) copy-start(bf16[256,64]{0,1:T(8,128)(2,1)} %param.16) | copy-start | bytes 98308
  43.0 7.0 %copy-start.3 = (bf16[2,128,512]{2,1,0:T(8,128)(2,1)S(1)}, bf16[2,128,512]{2,1,0:T(8,128)(2,1)}, u32[]{:S(2)}) copy-start(bf16[2,128,512]{2,1,0:T(8,128)(2,1)} %param.20) | copy-start | bytes 786436
  43.0 7.2 %copy-start.4 = (bf16[2,128,128]{2,1,0:T(8,128)(2,1)S(1)}, bf16[2,128,128]{2,1,0:T(8,128)(2,1)}, u32[]{:S(2)}) copy-start(bf16[2,128,128]{2,1,0:T(8,128)(2,1)} %param.21) | copy-start | bytes 196612
  43.0 7.3 %copy-start.5 = (bf16[2,128,128]{2,1,0:T(8,128)(2,1)S(1)}, bf16[2,128,128]{2,1,0:T(8,128)(2,1)}, u32[]{:S(2)}) copy-start(bf16[2,128,128]{2,1,0:T(8,128)(2,1)} %param.23) | copy-start | bytes 196612
  43.0 8.0 %copy-start.6 = (s32[32,256]{1,0:T(8,128)S(1)}, s32[32,256]{1,0:T(8,128)}, u32[]{:S(2)}) copy-start(s32[32,256]{1,0:T(8,128)} %param.13) | copy-start | bytes 98308
  43.0 10.9 %copy-start.9 = (f32[2,2,128]{2,1,0:T(2,128)S(1)}, f32[2,2,128]{2,1,0:T(2,128)}, u32[]{:S(2)}) copy-start(f32[2,2,128]{2,1,0:T(2,128)} %param.19) | copy-start | bytes 6148
  43.0 10.9 %copy-start.10 = (f32[2,2,128]{2,1,0:T(2,128)S(1)}, f32[2,2,128]{2,1,0:T(2,128)}, u32[]{:S(2)}) copy-start(f32[2,2,128]{2,1,0:T(2,128)} %param.22) | copy-start | bytes 6148
  114.9 16.3 %copy-start.2 = (f32[32,256,128]{1,2,0:T(8,128)S(1)}, f32[32,256,128]{1,2,0:T(8,128)}, u32[]{:S(2)}) copy-start(f32[32,256,128]{1,2,0:T(8,128)} %copy.42) | copy-start | bytes 12582916
  114.9 16.3 %copy-start.7 = (f32[128]{0:T(128)S(1)}, f32[128]{0:T(128)}, u32[]{:S(2)}) copy-start(f32[128]{0:T(128)} %param.18) | copy-start | bytes 1540
Sparse Core Ops, SparseCore 0:
  44.3 50.9 all-gather.1

commit v2 on v1

--- a/solution.py
+++ b/solution.py
@@ -10,26 +10,6 @@
 LN_EPS = 1e-5
 LANES = 128
 MESH = pl.DeviceIdType.MESH
-
-
-def norm_over(values, norm_scale, norm_shift, norm_axis):
-    chan_mean = jnp.mean(values, axis=norm_axis, keepdims=True)
-    centered = values - chan_mean
-    chan_var = jnp.mean(centered * centered, axis=norm_axis, keepdims=True)
-    return (centered * lax.rsqrt(chan_var + LN_EPS) * norm_scale + norm_shift).astype(jnp.bfloat16)
-
-
-def outer_product_mean(value_a7, opm_norm, opm_proj, opm_out, opm_bias):
-    value_a9 = value_a7.shape[0]
-    opm_dim = opm_proj.shape[1] // 2
-    value_a8 = norm_over(value_a7.astype(jnp.float32), opm_norm[0], opm_norm[1], -1)
-    proj_all = jnp.einsum("srm,mp->srp", value_a8, opm_proj, preferred_element_type=jnp.float32).astype(jnp.bfloat16)
-    right_full = lax.all_gather(proj_all[:, :, opm_dim:], "dap", axis=1, tiled=True)
-    outer_prod = jnp.einsum("sip,sjq->ijpq", proj_all[:, :, :opm_dim], right_full, preferred_element_type=jnp.float32) / value_a9
-    local_rows = outer_prod.shape[0]
-    residues = outer_prod.shape[1]
-    outer_flat = outer_prod.astype(jnp.bfloat16).reshape(local_rows, residues, opm_dim * opm_dim)
-    return jnp.einsum("ijf,fz->ijz", outer_flat, opm_out, preferred_element_type=jnp.float32) + opm_bias
 
 
 def _col(v, n):
@@ -60,7 +40,6 @@
     halves = cols // LANES
     pst = st.shape[2] // ch_rows
     pxt = tb.shape[1] // chan
-    slot = ch_rows
 
     def zcopy(ch):
         at = pl.ds(ch * ch_rows, ch_rows)
@@ -70,7 +49,7 @@
         buf = rb if t else ra
         return pltpu.make_async_remote_copy(
             src_ref=snd.at[t, ch, pl.ds(pl.multiple_of(dst * cown, cown), cown)],
-            dst_ref=buf.at[src, :, pl.ds(ch * slot, slot)],
+            dst_ref=buf.at[ch, src],
             send_sem=ss_ab.at[t, ch, dst], recv_sem=rs_ab.at[t, ch, src],
             device_id={"dap": dst}, device_id_type=MESH)
 
@@ -118,8 +97,8 @@
         for t, k in order:
             for s in range(1, n):
                 ab_copy(t, k, me, lax.rem(me + s, n)).start()
-        ra[me, :, ch * slot:(ch + 1) * slot] = snd[0, ch, own]
-        rb[me, :, ch * slot:(ch + 1) * slot] = snd[1, ch, own]
+        ra[ch, me] = snd[0, ch, own]
+        rb[ch, me] = snd[1, ch, own]
 
     def wait_ab(t, ch):
         for s in range(1, n):
@@ -138,11 +117,11 @@
 
         @pl.loop(0, cown)
         def _(c):
-            x = lax.dot_general(ra[:, c].reshape(n * rows, cols), rb[:, c].reshape(n * rows, cols),
+            x = lax.dot_general(ra[:, :, c].reshape(n * rows, cols), rb[:, :, c].reshape(n * rows, cols),
                                 (((0,), (0,)), ((), ())), preferred_element_type=jnp.float32)
-            x = x.astype(jnp.bfloat16).reshape(n, chunks, ch_rows, cols)
+            x = x.astype(jnp.bfloat16).reshape(chunks, n, ch_rows, cols)
             for ch in range(chunks):
-                xs[ch, :, c] = x[:, ch]
+                xs[ch, :, c] = x[ch]
         for ch in range(chunks):
             send_x(ch)
     else:
@@ -151,8 +130,8 @@
 
             @pl.loop(0, cown)
             def _(c, ch=ch):
-                x = lax.dot_general(ra[:, c, ch * slot:(ch + 1) * slot].reshape(n * ch_rows, cols),
-                                    rb[:, c].reshape(n * rows, cols),
+                x = lax.dot_general(ra[ch, :, c].reshape(n * ch_rows, cols),
+                                    rb[:, :, c].reshape(n * rows, cols),
                                     (((1,), (1,)), ((), ())), preferred_element_type=jnp.float32)
                 xs[ch, :, c] = x.astype(jnp.bfloat16).reshape(n, ch_rows, cols)
             send_x(ch)
@@ -173,7 +152,11 @@
             x = jnp.concatenate([tb[h, pl.ds(i, chan, stride=pxt), :] for h in range(halves)], axis=1)
             xn = _norm_rows(x, xscale, xshift)
             upd = jnp.dot(wout_ref[...], xn, preferred_element_type=jnp.float32)
-            ob[r] = zb[r] + gb[r] * upd
+            new = zb[r] + gb[r] * upd
+            if incoming:
+                ob[r] = new.T.reshape(chunks, n, cols // (chunks * n), chan).swapaxes(0, 1).reshape(cols, chan)
+            else:
+                ob[r] = new
         at = pl.ds(ch * ch_rows, ch_rows)
         pltpu.make_async_copy(ob.at[at], o_hbm.at[at], osem.at[ch]).start()
 
@@ -193,13 +176,14 @@
     chunks = 2
     ch_rows = rows // chunks
     halves = cols // LANES
+    out_block = (rows, cols, chan) if incoming else z_cm.shape
     w_all = jnp.concatenate([w_proj, w_gate], axis=1).T
     nrm = jnp.stack([_col(norm_pair[0], cols), _col(norm_pair[1], cols), _col(norm_mix[0], cols), _col(norm_mix[1], cols)])
     vm = pl.BlockSpec(memory_space=pltpu.VMEM)
     hbm = pl.BlockSpec(memory_space=pl.ANY)
     return pl.pallas_call(
         functools.partial(_tri_kernel, n, incoming),
-        out_shape=jax.ShapeDtypeStruct(z_cm.shape, jnp.float32),
+        out_shape=jax.ShapeDtypeStruct(out_block, jnp.float32),
         in_specs=[hbm, vm, vm, vm, vm],
         out_specs=hbm,
         scratch_shapes=[
@@ -207,12 +191,12 @@
             pltpu.VMEM((rows, chan, cols), jnp.float32),
             pltpu.VMEM((2, halves, ch_rows * (chan + 8), LANES), jnp.float32),
             pltpu.VMEM((2, chunks, chan, ch_rows, cols), jnp.bfloat16),
-            pltpu.VMEM((n, cown, rows, cols), jnp.bfloat16),
-            pltpu.VMEM((n, cown, rows, cols), jnp.bfloat16),
+            pltpu.VMEM((chunks, n, cown, ch_rows, cols), jnp.bfloat16),
+            pltpu.VMEM((chunks, n, cown, ch_rows, cols), jnp.bfloat16),
             pltpu.VMEM((chunks, n, cown, ch_rows, cols), jnp.bfloat16),
             pltpu.VMEM((chunks, chan, ch_rows, cols), jnp.bfloat16),
             pltpu.VMEM((halves, chan * (ch_rows + 8), LANES), jnp.float32),
-            pltpu.VMEM((rows, chan, cols), jnp.float32),
+            pltpu.VMEM(out_block, jnp.float32),
             pltpu.SemaphoreType.DMA((chunks,)),
             pltpu.SemaphoreType.DMA((chunks,)),
             pltpu.SemaphoreType.DMA((2, chunks, n)),
@@ -225,6 +209,192 @@
     )(z_cm, mask_f, w_all, w_out.T, nrm)
 
 
+def _opm_kernel(n, z_hbm, msa_hbm, nrm_ref, proj_ref, wt_ref, bias_ref, o_hbm,
+                mb, ub, at_b, bt, ball, obuf, zi, zo, msem, zsem, osem, ss, rs):
+    me = lax.axis_index("dap")
+    depth, grp, mdim = mb.shape[1:]
+    rows = zi.shape[0]
+    groups = rows // grp
+    chunks, odim, lanes = ball.shape[:3]
+    jrows = lanes // n
+    per = jrows // grp
+    qh = odim // 2
+    pst = bt.shape[1] // jrows
+    tiles = depth // LANES
+    part = me + 1 - 2 * lax.rem(me, 2)
+    right, left, opp = lax.rem(me + 2, n), lax.rem(me + n - 2, n), lax.rem(me + 4, n)
+
+    def mcopy(g):
+        return pltpu.make_async_copy(msa_hbm.at[:, pl.ds(g * grp, grp)], mb.at[g % 2], msem.at[g % 2])
+
+    def block(c, h, src):
+        return ball.at[c, h * qh:(h + 1) * qh, pl.ds(pl.multiple_of(src * jrows, jrows), jrows)]
+
+    def send(c, h, src, k, dst):
+        return pltpu.make_async_remote_copy(
+            src_ref=block(c, h, src), dst_ref=block(c, h, src), send_sem=ss.at[c, h, k], recv_sem=rs.at[c, h, src],
+            device_id={"dap": dst}, device_id_type=MESH)
+
+    def arrived(c, h, src):
+        send(c, h, src, 0, part).wait_recv()
+
+    mcopy(0).start()
+    mcopy(1).start()
+    zcopy = pltpu.make_async_copy(z_hbm, zi, zsem.at[0])
+    zcopy.start()
+    _entry_barrier(me, n)
+
+    scale, shift = nrm_ref[0:1, :], nrm_ref[1:2, :]
+    sb = 32
+
+    def project(c):
+        for k in range(per):
+            g = c * per + k
+            mcopy(g).wait()
+
+            @pl.loop(0, depth // sb)
+            def _(b, g=g):
+                x = mb[g % 2, pl.ds(b * sb, sb)].astype(jnp.float32).reshape(sb * grp, mdim)
+                mean = jnp.mean(x, axis=1, keepdims=True)
+                cen = x - mean
+                var = jnp.mean(cen * cen, axis=1, keepdims=True)
+                y = (cen * lax.rsqrt(var + LN_EPS) * scale + shift).astype(jnp.bfloat16)
+                ub[pl.ds(pl.multiple_of(b * (sb * grp), sb * grp), sb * grp), :] = jnp.dot(y, proj_ref[...], preferred_element_type=jnp.float32)
+            if g + 2 < groups:
+                mcopy(g + 2).start()
+
+            @pl.loop(0, grp)
+            def _(i, g=g, k=k):
+                v = ub[pl.ds(i, depth, stride=grp), :].T
+                r = g * grp + i
+                at_b[pl.ds(pl.multiple_of(r * odim, odim), odim), :] = v[:odim].astype(jnp.bfloat16)
+                row = pl.multiple_of((k * grp + i) * pst, 8)
+                for t in range(tiles):
+                    bt[t, pl.ds(row, odim), :] = v[odim:2 * odim, t * LANES:(t + 1) * LANES]
+
+        @pl.loop(0, odim, unroll=4)
+        def _(q):
+            for t in range(tiles):
+                ball[c, q, pl.ds(pl.multiple_of(me * jrows, jrows), jrows), t * LANES:(t + 1) * LANES] = (
+                    bt[t, pl.ds(q, jrows, stride=pst), :].astype(jnp.bfloat16))
+
+    def send_own(c):
+        for h in (0, 1):
+            send(c, h, me, 0, right).start()
+            send(c, 1 - h, me, 1, left).start()
+        for h in (0, 1):
+            send(c, h, me, 2, part).start()
+
+    def forward_far(c):
+        arrived(c, 0, left)
+        send(c, 0, left, 3, right).start()
+        send(c, 0, left, 4, part).start()
+        arrived(c, 1, right)
+        send(c, 1, right, 3, left).start()
+        send(c, 1, right, 4, part).start()
+
+    def forward_near(c):
+        arrived(c, 1, left)
+        send(c, 1, left, 5, part).start()
+        arrived(c, 0, right)
+        send(c, 0, right, 5, part).start()
+
+    def forward_opp(c):
+        for h in (0, 1):
+            arrived(c, h, opp)
+            send(c, h, opp, 6, part).start()
+
+    def partner_all(c):
+        for d in (0, 2, 4, 6):
+            src = lax.rem(part + d, n)
+            for h in (0, 1):
+                arrived(c, h, src)
+
+    def outer(c, lo, hi):
+        @pl.loop(lo, hi)
+        def _(b):
+            rhs = ball[c, pl.ds(b * 2, 2)].reshape(2 * lanes, depth)
+            o = lax.dot_general(at_b[...], rhs, (((1,), (1,)), ((), ())), preferred_element_type=jnp.float32)
+            o = (o * (1.0 / depth)).astype(jnp.bfloat16)
+            for t in range(2):
+                obuf[b * 2 + t] = o[:, t * lanes:(t + 1) * lanes]
+
+    def mix(c, lo, hi):
+        @pl.loop(lo, hi)
+        def _(i):
+            rhs = obuf[:, pl.ds(pl.multiple_of(i * odim, odim), odim), :].reshape(odim * odim, lanes)
+            upd = jnp.dot(wt_ref[...], rhs, preferred_element_type=jnp.float32)
+            zt = zi[i].reshape(n, chunks, jrows, zi.shape[2])[:, c].reshape(lanes, zi.shape[2]).T
+            zo[i, :, c * lanes:(c + 1) * lanes] = zt + (upd + bias_ref[...])
+
+    blocks = odim // 2
+    project(0)
+    send_own(0)
+    project(1)
+    forward_far(0)
+    send_own(1)
+    forward_near(0)
+    forward_opp(0)
+    partner_all(0)
+    outer(0, 0, blocks // 2)
+    forward_far(1)
+    outer(0, blocks // 2, blocks)
+    zcopy.wait()
+    forward_near(1)
+    mix(0, 0, rows)
+    forward_opp(1)
+    partner_all(1)
+    outer(1, 0, blocks)
+    half = rows // 2
+    for k in range(2):
+        mix(1, k * half, (k + 1) * half)
+        pltpu.make_async_copy(zo.at[pl.ds(k * half, half)], o_hbm.at[pl.ds(k * half, half)], osem.at[k]).start()
+    for k in range(2):
+        pltpu.make_async_copy(zo.at[pl.ds(k * half, half)], o_hbm.at[pl.ds(k * half, half)], osem.at[k]).wait()
+    for c in range(chunks):
+        for h in (0, 1):
+            for k, src in ((0, me), (1, me), (2, me), (3, left if h == 0 else right), (4, left if h == 0 else right),
+                           (5, right if h == 0 else left), (6, opp)):
+                send(c, h, src, k, part).wait_send()
+
+
+def _opm_call(n, pair_loc, msa, opm_norm, opm_proj, opm_out, opm_bias):
+    rows, cols, chan = pair_loc.shape
+    depth, _, mdim = msa.shape
+    odim = opm_proj.shape[1] // 2
+    grp = 8
+    chunks = 2
+    lanes = cols // chunks
+    proj = jnp.pad(opm_proj, ((0, 0), (0, LANES - 2 * odim)))
+    wt = opm_out.reshape(odim, odim, chan).transpose(2, 1, 0).reshape(chan, odim * odim)
+    vm = pl.BlockSpec(memory_space=pltpu.VMEM)
+    hbm = pl.BlockSpec(memory_space=pl.ANY)
+    jrows = lanes // n
+    return pl.pallas_call(
+        functools.partial(_opm_kernel, n),
+        out_shape=jax.ShapeDtypeStruct((rows, chan, cols), jnp.float32),
+        in_specs=[hbm, hbm, vm, vm, vm, vm],
+        out_specs=hbm,
+        scratch_shapes=[
+            pltpu.VMEM((2, depth, grp, mdim), jnp.bfloat16),
+            pltpu.VMEM((depth * grp, LANES), jnp.float32),
+            pltpu.VMEM((rows * odim, depth), jnp.bfloat16),
+            pltpu.VMEM((depth // LANES, jrows * (odim + 8), LANES), jnp.float32),
+            pltpu.VMEM((chunks, odim, lanes, depth), jnp.bfloat16),
+            pltpu.VMEM((odim, rows * odim, lanes), jnp.bfloat16),
+            pltpu.VMEM((rows, cols, chan), jnp.float32),
+            pltpu.VMEM((rows, chan, cols), jnp.float32),
+            pltpu.SemaphoreType.DMA((2,)),
+            pltpu.SemaphoreType.DMA((1,)),
+            pltpu.SemaphoreType.DMA((2,)),
+            pltpu.SemaphoreType.DMA((chunks, 2, 7)),
+            pltpu.SemaphoreType.DMA((chunks, 2, n)),
+        ],
+        compiler_params=pltpu.CompilerParams(collective_id=3, has_side_effects=True, vmem_limit_bytes=60 * 1024 * 1024),
+        name="opm",
+    )(pair_loc, msa, opm_norm, proj, wt, _col(opm_bias, lanes))
+
+
 def solution(mesh):
     row_spec = P(("data", "dap"), None, None)
     mask_spec = P(("data", "dap"), None)
@@ -233,11 +403,11 @@
 
     def local_program(pair_loc, mask_loc, value_a7, opm_norm, opm_proj, opm_out, opm_bias, tri_norm, tri_proj, tri_gate, tri_xnorm, tri_out):
         n = lax.axis_size("dap")
-        mask_f = mask_loc.astype(jnp.float32)
-        pair_zero = pair_loc + outer_product_mean(value_a7, opm_norm, opm_proj, opm_out, opm_bias)
-        z = jnp.swapaxes(pair_zero, 1, 2)
+        rows, cols = mask_loc.shape
+        mask_f = mask_loc.astype(jnp.float32).reshape(rows, n, 2, cols // (2 * n)).swapaxes(1, 2).reshape(rows, cols)
+        z = _opm_call(n, pair_loc, value_a7, opm_norm, opm_proj, opm_out, opm_bias)
         for t in range(2):
             z = _tri_call(n, t == 1, z, mask_f, tri_proj[t], tri_gate[t], tri_norm[t], tri_xnorm[t], tri_out[t])
-        return jnp.swapaxes(z, 1, 2)
+        return z
 
     return jax.shard_map(local_program, mesh=mesh, in_specs=(row_spec, mask_spec, array_b8) + (replicated,) * 9, out_specs=row_spec, check_vma=False)

time: 324 us -> 272 us (0.84)
  Pallas kernels: 175 us -> 252 us
  waiting for transfers between devices: 39 us -> 0 us
  matrix products: 34 us -> 0 us
  other arithmetic: 30.7 us -> 3.1 us
  local copies, waits for them, and re-layouts: 31.3 us -> 16.2 us
  between operations: 13.7 us -> 0.14 us
    pallas_call x0 -> x1, Pallas kernels: none -> 76.8 us  [_opm_call(): pl.pallas_call(functools.partial(_opm_kernel, n), out_shape=jax.ShapeDtyp...]
    all_gather x1 -> x0, waiting for transfers between devices: 38.9 us -> none  [outer_product_mean(): lax.all_gather(proj_all[:, :, opm_dim:], 'dap', axis=1, tiled=True)]
    dot_general x3 -> x0, matrix products: 34 us -> none  [the longest x1 19.6 us: outer_product_mean(): jnp.einsum('sip,sjq->ijpq', proj_all[:, :, :opm_dim], right_full, preferr...]
    reduce_sum x2 -> x0, other arithmetic: 19.6 us -> none  [the longest x1 13.8 us: norm_over(): chan_var = jnp.mean(centered * centered, axis=norm_axis, keepdims=True)]
    convert_element_type x1 -> x0, local copies, waits for them, and re-layouts: 16.3 us -> none  [outer_product_mean(): outer_prod.astype(jnp.bfloat16)]
    convert_element_type x2 -> x1, other arithmetic: 7.9 us -> 0.01 us  [local_program(): mask_loc.astype(jnp.float32).reshape(rows, n, 2, cols // (2 * n))]
    transpose x1 -> x2, local copies, waits for them, and re-layouts: 5.57 us -> 1.06 us  [the longest x1 1.05 us: _opm_call(): opm_out.reshape(odim, odim, chan).transpose(2, 1, 0)]
    unnamed x31 -> x13, local copies, waits for them, and re-layouts: 7.78 us -> 7.53 us
  transfers between devices with their start and end apart: 1 -> 0, of which waited for: 1 -> 0; matrix products, arithmetic and copies ran while one was open for 4% -> 0% of each run, Pallas kernels for 0% -> 0%
where the time goes in v2:
time: 272 us
  Pallas kernels  252 us (93%)
  local copies, waits for them, and re-layouts  16.2 us (6%)
  other arithmetic  3.1 us (1%)
    pallas_call x2, Pallas kernels, _tri_call(): pl.pallas_call(functools.partial(_tri_kernel, n, incoming), out_shape=jax...  176 us
    pallas_call x1, Pallas kernels, _opm_call(): pl.pallas_call(functools.partial(_opm_kernel, n), out_shape=jax.ShapeDtyp...  76.8 us
    unnamed x13, local copies, waits for them, and re-layouts  7.53 us

profile of v2, /device:TPU:81, one launch (start us, length us, event | category | flops | bytes accessed | tf_op | source)
XLA Modules:
  0.0 271.8 jit_solution(4157693239230397999)
XLA Ops:
  0.0 0.0 copy-start
  0.0 0.0 copy-start.1
  0.0 0.8 slice_bitcast_fusion.3
  0.8 0.1 stack_broadcast_in_dim.57
  0.8 0.1 stack_broadcast_in_dim.59
  0.9 0.8 slice_bitcast_fusion.1
  1.7 0.1 stack_broadcast_in_dim.61
  1.8 0.1 stack_broadcast_in_dim.63
  1.9 0.8 pad_maximum_fusion.nrm_ref
  2.7 1.0 fusion
  3.7 0.1 copy.47
  3.8 0.8 fusion.2
  4.6 0.1 copy.48
  4.7 0.7 maximum_bitcast_fusion.w_ref
  5.4 0.9 copy.37
  6.3 0.7 copy.42.mask_ref
  7.0 0.8 fusion.1
  7.8 0.7 copy.49
  8.5 1.1 copy.35
  9.6 0.8 copy.36.wt_ref
  10.4 0.0 copy-done
  10.4 0.1 copy.34
  10.5 0.6 pad.4.proj_ref
  11.2 0.0 copy-done.1
  11.2 0.7 broadcast_in_dim.2.bias_ref
  11.9 76.8 %opm.1.z_hbm = f32[32,128,256]{2,1,0:T(8,128)} custom-call(f32[32,256,128]{2,1,0:T(8,128)} %z_hbm.1, bf16[512,32,256]{2,1,0:T(8,128)(2,1)} %msa_hbm.1, f32[2,256]{1,0:T(2,128)} %nrm_ref.1, bf16[256,128]{1,0:T(8,128)(2,1)} %pad.4.proj_ref, bf16[128,1024]{1,0:T(8,128)(2,1)} %copy.36.wt_ref, f32[128,128]{1,0:T(8,128)} %broadcast_in_dim.2.bias_ref), custom_call_target="tpu_custom_call" | custom-call | tf_op jit(solution)/shard_map/opm/pallas_call | solution.py:373
  88.8 84.7 %tri_out.1.z_hbm = f32[32,128,256]{2,1,0:T(8,128)} custom-call(f32[32,128,256]{2,1,0:T(8,128)} %opm.1.z_hbm, f32[32,256]{1,0:T(8,128)} %copy.42.mask_ref, bf16[640,128]{1,0:T(8,128)(2,1)} %maximum_bitcast_fusion.w_ref, bf16[128,128]{1,0:T(8,128)(2,1)} %bitcast.44, f32[4,128,256]{2,1,0:T(8,128)} %pad_maximum_fusion.nrm_ref), custom_call_target="tpu_custom_call" | custom-call | tf_op jit(solution)/shard_map/tri_out/pallas_call | solution.py:184
  173.5 0.1 stack_broadcast_in_dim.65
  173.6 0.1 stack_broadcast_in_dim.67
  173.6 0.1 stack_broadcast_in_dim.69
  173.7 0.1 stack_broadcast_in_dim.71
  173.8 0.8 pad_maximum_fusion.1.nrm_ref
  174.7 0.1 copy.50
  174.8 0.1 copy.51
  174.9 0.7 maximum_bitcast_fusion.1.w_ref
  175.6 0.7 copy.52
  176.3 90.8 %tri_in.1 = f32[32,256,128]{2,1,0:T(8,128)} custom-call(f32[32,128,256]{2,1,0:T(8,128)} %tri_out.1.z_hbm, f32[32,256]{1,0:T(8,128)} %copy.42.mask_ref, bf16[640,128]{1,0:T(8,128)(2,1)} %maximum_bitcast_fusion.1.w_ref, bf16[128,128]{1,0:T(8,128)(2,1)} %bitcast.45, f32[4,128,256]{2,1,0:T(8,128)} %pad_maximum_fusion.1.nrm_ref), custom_call_target="tpu_custom_call" | custom-call | tf_op jit(solution)/shard_map/tri_in/pallas_call | solution.py:184
  267.2 4.7 %copy.54 = f32[32,256,128]{2,1,0:T(8,128)} copy(f32[32,256,128]{2,1,0:T(8,128)} %tri_in.1) | data formatting | bytes 8388608
  (2 shorter events, 0.0 us)
Async XLA Ops:
  0.0 10.4 %copy-start = (bf16[256,64]{0,1:T(8,128)(2,1)S(1)}, bf16[256,64]{0,1:T(8,128)(2,1)}, u32[]{:S(2)}) copy-start(bf16[256,64]{0,1:T(8,128)(2,1)} %param.16) | copy-start | bytes 98308
  0.0 11.2 %copy-start.1 = (f32[128]{0:T(128)S(1)}, f32[128]{0:T(128)}, u32[]{:S(2)}) copy-start(f32[128]{0:T(128)} %param.18) | copy-start | bytes 1540

commit v3 on v0

v3 whole, which is shorter than its diff:
```python
import functools

import jax
import jax.numpy as jnp
from jax import lax
from jax.experimental import pallas as pl
from jax.experimental.pallas import tpu as pltpu
from jax.sharding import PartitionSpec as P

LN_EPS = 1e-5
LANES = 128
TILE = 16
MESH = pl.DeviceIdType.MESH


def _norm_rows(v, scale, shift):
    mean = jnp.mean(v, axis=0, keepdims=True)
    cen = v - mean
    var = jnp.mean(cen * cen, axis=0, keepdims=True)
    return (cen * lax.rsqrt(var + LN_EPS) * scale + shift).astype(jnp.bfloat16)


def _column(row, n):
    return jnp.broadcast_to(row, (n, row.shape[1])).T


def _kernel(n, z_hbm, mask_ref, msa_hbm, onrm_ref, oproj_ref, oout_ref, obias_ref, nrm_ref, proj_ref, gate_ref, xnrm_ref, out_ref, o_hbm,
            mb, fb, at_b, ball, obuf, zi, zb, gb, st, snd, ra, rb, xs, xr, mk, wt, wa, wo, nc, bc,
            msem, zsem, osem, ss, rs, ss_ab, rs_ab, ss_x, rs_x):
    me = lax.axis_index("dap")
    depth, grp, mdim = mb.shape[1:]
    rows, cols, chan = zi.shape
    chunks, odim, lanes = ball.shape[:3]
    jrows = lanes // n
    groups = rows // grp
    per = jrows // grp
    qh = odim // 2
    cown = chan // n
    blocks = odim // 2
    tiles = depth // LANES
    bst, pst, pxt = odim + 8, chan + 8, jrows + 8
    part = me + 1 - 2 * lax.rem(me, 2)
    right, left, opp = lax.rem(me + 2, n), lax.rem(me + n - 2, n), lax.rem(me + 4, n)

    def mcopy(g):
        return pltpu.make_async_copy(msa_hbm.at[:, pl.ds(g * grp, grp)], mb.at[g % 2], msem.at[g % 2])

    mcopy(0).start()
    mcopy(1).start()
    zcopy = pltpu.make_async_copy(z_hbm, zi, zsem.at[0])
    zcopy.start()
    barrier = pltpu.get_barrier_semaphore()
    for s in range(1, n):
        pl.semaphore_signal(barrier, inc=1, device_id={"dap": lax.rem(me + s, n)}, device_id_type=MESH)
    pl.semaphore_wait(barrier, n - 1)

    def block(c, h, src):
        return ball.at[c, h * qh:(h + 1) * qh, pl.ds(pl.multiple_of(src * jrows, jrows), jrows)]

    def send(c, h, src, k, dst):
        return pltpu.make_async_remote_copy(
            src_ref=block(c, h, src), dst_ref=block(c, h, src), send_sem=ss.at[c, h, k], recv_sem=rs.at[c, h, src],
            device_id={"dap": dst}, device_id_type=MESH)

    def arrived(c, h, src):
        send(c, h, src, 0, part).wait_recv()

    oscale, oshift = onrm_ref[0:1, :], onrm_ref[1:2, :]
    sb = 64

    def project(c):
        for k in range(per):
            g = c * per + k
            mcopy(g).wait()

            @pl.loop(0, depth // sb)
            def _(b, g=g):
                x = mb[g % 2, pl.ds(b * sb, sb)].astype(jnp.float32).reshape(sb * grp, mdim)
                mean = jnp.mean(x, axis=1, keepdims=True)
                cen = x - mean
                var = jnp.mean(cen * cen, axis=1, keepdims=True)
                y = (cen * lax.rsqrt(var + LN_EPS) * oscale + oshift).astype(jnp.bfloat16)
                at = pl.ds(pl.multiple_of(b * (sb * grp), sb * grp), sb * grp)
                fb[at, :2 * odim] = jnp.dot(y, oproj_ref[...], preferred_element_type=jnp.float32)
            if g + 2 < groups:
                mcopy(g + 2).start()

            @pl.loop(0, grp)
            def _(i, g=g, k=k):
                v = fb[pl.ds(i, depth, stride=grp), :].T
                r = g * grp + i
                at_b[pl.ds(pl.multiple_of(r * odim, odim), odim), :] = v[:odim].astype(jnp.bfloat16)
                for t in range(tiles):
                    row = pl.multiple_of(t * (jrows * bst) + (k * grp + i) * bst, 8)
                    st[pl.ds(row, odim), :] = v[odim:2 * odim, t * LANES:(t + 1) * LANES]

        @pl.loop(0, odim, unroll=4)
        def _(q):
            for t in range(tiles):
                ball[c, q, pl.ds(pl.multiple_of(me * jrows, jrows), jrows), t * LANES:(t + 1) * LANES] = (
                    st[pl.ds(t * (jrows * bst) + q, jrows, stride=bst), :].astype(jnp.bfloat16))

    def send_own(c):
        for h in (0, 1):
            send(c, h, me, 0, right).start()
            send(c, 1 - h, me, 1, left).start()
        for h in (0, 1):
            send(c, h, me, 2, part).start()

    def forward_far(c):
        arrived(c, 0, left)
        send(c, 0, left, 3, right).start()
        send(c, 0, left, 4, part).start()
        arrived(c, 1, right)
        send(c, 1, right, 3, left).start()
        send(c, 1, right, 4, part).start()

    def forward_near(c):
        arrived(c, 1, left)
        send(c, 1, left, 5, part).start()
        arrived(c, 0, right)
        send(c, 0, right, 5, part).start()

    def forward_opp(c):
        for h in (0, 1):
            arrived(c, h, opp)
            send(c, h, opp, 6, part).start()

    def partner_all(c):
        for d in (0, 2, 4, 6):
            for h in (0, 1):
                arrived(c, h, lax.rem(part + d, n))

    def outer(c, lo, hi):
        @pl.loop(lo, hi)
        def _(b):
            rhs = ball[c, pl.ds(b * 2, 2)].reshape(2 * lanes, depth)
            o = lax.dot_general(at_b[...], rhs, (((1,), (1,)), ((), ())), preferred_element_type=jnp.float32)
            o = (o * (1.0 / depth)).astype(jnp.bfloat16)
            nt = rows * odim // TILE
            for t in range(2):
                obuf[b, t * nt:(t + 1) * nt] = o[:, t * lanes:(t + 1) * lanes].reshape(nt, TILE, lanes)

    def mix(c):
        @pl.loop(0, rows)
        def _(i):
            nt, w = rows * odim // TILE, odim // TILE
            rhs = jnp.stack([obuf[:, pl.ds(t * nt + i * w, w)] for t in range(2)], axis=1).reshape(odim * odim, lanes)
            upd = jnp.dot(wt[...], rhs, preferred_element_type=jnp.float32)
            zt = zi[i].reshape(n, chunks, jrows, chan)[:, c].reshape(lanes, chan).T
            zb[i, :, c * lanes:(c + 1) * lanes] = zt + (upd + bc[...])

    def prepare():
        rid = lax.broadcasted_iota(jnp.int32, (cols, cols), 0)
        cid = lax.broadcasted_iota(jnp.int32, (cols, cols), 1)
        two = chunks * jrows
        place = ((rid // jrows) % chunks) * lanes + (rid // two) * jrows + rid % jrows
        perm = (cid == place).astype(jnp.float32).astype(jnp.bfloat16)
        mk[...] = jnp.dot(mask_ref[...].astype(jnp.float32).astype(jnp.bfloat16), perm, preferred_element_type=jnp.float32)
        bc[...] = _column(obias_ref[...], lanes)
        for t in range(2):
            for k in range(2):
                nc[t, k] = _column(nrm_ref[t, k:k + 1, :], lanes)
                nc[t, 2 + k] = _column(xnrm_ref[t, k:k + 1, :], lanes)
            for k in range(4):
                wa[t, k * chan:(k + 1) * chan] = proj_ref[t, :, k * chan:(k + 1) * chan].astype(jnp.float32).T.astype(jnp.bfloat16)
            wa[t, 4 * chan:] = gate_ref[t].astype(jnp.float32).T.astype(jnp.bfloat16)
            wo[t] = out_ref[t].astype(jnp.float32).T.astype(jnp.bfloat16)
        fb[:odim * odim, :] = oout_ref[...].astype(jnp.float32)

        @pl.loop(0, odim * odim // LANES)
        def _(b):
            m = LANES // odim
            v = jnp.concatenate([fb[pl.ds(b * m + k, odim, stride=odim), :] for k in range(m)], axis=0)
            wt[:, pl.ds(pl.multiple_of(b * LANES, LANES), LANES)] = v.T.astype(jnp.bfloat16)

    def piece_rows(u, pieces):
        @pl.loop(0, jrows)
        def _(i):
            at = [(r0 + i, h * lanes) for r0, h in pieces]
            z = jnp.concatenate([zb[r, :, h:h + lanes] for r, h in at], axis=1)
            m = jnp.concatenate([mk[pl.ds(r, 1), :][:, h:h + lanes] for r, h in at], axis=1)
            scale = jnp.concatenate([nc[u, 0]] * 2, axis=1)
            shift = jnp.concatenate([nc[u, 1]] * 2, axis=1)
            q = jnp.dot(wa[u], _norm_rows(z, scale, shift), preferred_element_type=jnp.float32)
            ab = (m * jax.nn.sigmoid(q[chan:2 * chan]) * q[:chan], m * jax.nn.sigmoid(q[3 * chan:4 * chan]) * q[2 * chan:3 * chan])
            g = jax.nn.sigmoid(q[4 * chan:])
            for s, (r, h) in enumerate(at):
                gb[r, :, h:h + lanes] = g[:, s * lanes:(s + 1) * lanes]
                for t in range(2):
                    st[pl.ds(pl.multiple_of((t * 2 + s) * (jrows * pst) + i * pst, 8), chan), :] = ab[t][:, s * lanes:(s + 1) * lanes]

    def turn(p):
        @pl.loop(0, chan, unroll=8)
        def _(c):
            for t in range(2):
                for s in range(2):
                    snd[t, p, s, c] = st[pl.ds((t * 2 + s) * (jrows * pst) + c, jrows, stride=pst), :].astype(jnp.bfloat16)

    own = pl.ds(pl.multiple_of(me * cown, cown), cown)

    def landing(u, t, p, s, src):
        if u == 0:
            return (rb if t else ra).at[p, s, src]
        return obuf.at[t * 4 + p * 2 + s, pl.ds(pl.multiple_of(src * cown, cown), cown)]

    def ab_copy(u, t, p, s, src, dst):
        return pltpu.make_async_remote_copy(
            src_ref=snd.at[t, p, s, pl.ds(pl.multiple_of(dst * cown, cown), cown)], dst_ref=landing(u, t, p, s, src),
            send_sem=ss_ab.at[u, t, p, s, dst], recv_sem=rs_ab.at[u, t, p, s, src],
            device_id={"dap": dst}, device_id_type=MESH)

    def ab_send(u, t, p, s):
        for d in range(1, n):
            ab_copy(u, t, p, s, me, lax.rem(me + d, n)).start()
        landing(u, t, p, s, me)[...] = snd[t, p, s, own]

    def ab_wait(u, t, p, s):
        for d in range(1, n):
            ab_copy(u, t, p, s, lax.rem(me + d, n), me).wait_recv()

    def x_copy(u, p, src, dst):
        return pltpu.make_async_remote_copy(
            src_ref=xs.at[p, dst], dst_ref=xr.at[p, pl.ds(pl.multiple_of(src * cown, cown), cown)],
            send_sem=ss_x.at[u, p, dst], recv_sem=rs_x.at[u, p, src],
            device_id={"dap": dst}, device_id_type=MESH)

    def x_send(u, p):
        for d in range(1, n):
            x_copy(u, p, me, lax.rem(me + d, n)).start()
        xr[p, own] = xs[p, me]

    def x_wait(u, p):
        for d in range(1, n):
            x_copy(u, p, lax.rem(me + d, n), me).wait_recv()

    def sent(u):
        for d in range(1, n):
            dst = lax.rem(me + d, n)
            for t in range(2):
                for p in range(2):
                    for s in range(2):
                        ab_copy(u, t, p, s, me, dst).wait_send()

    def x_sent(u):
        for d in range(1, n):
            for p in range(2):
                x_copy(u, p, me, lax.rem(me + d, n)).wait_send()

    def x_out(p):
        @pl.loop(0, cown)
        def _(c):
            a = jnp.concatenate([ra[h, p, :, c].reshape(lanes, lanes) for h in range(2)], axis=1)
            b = jnp.concatenate([rb[h, :, :, c].reshape(cols, lanes) for h in range(2)], axis=1)
            x = lax.dot_general(a, b, (((1,), (1,)), ((), ())), preferred_element_type=jnp.float32)
            xs[p, :, c] = x.astype(jnp.bfloat16).reshape(n, jrows, cols)

    def x_in():
        @pl.loop(0, cown)
        def _(c):
            a, b = (jnp.concatenate([
                jnp.concatenate([obuf[t * 4 + p * 2 + s, src * cown + c] for p in range(2) for src in range(n)], axis=0)
                for s in range(2)], axis=1) for t in range(2))
            x = lax.dot_general(a, b, (((0,), (0,)), ((), ())), preferred_element_type=jnp.float32)
            x = x.astype(jnp.bfloat16).reshape(2, n, jrows, cols)
            for p in range(2):
                xs[p, :, c] = x[p]

    def finish(u, p):
        half = chan * pxt

        @pl.loop(0, chan, unroll=8)
        def _(c):
            for h in range(2):
                fb[pl.ds(pl.multiple_of(h * half + c * pxt, 8), jrows), :] = xr[p, c, :, h * lanes:(h + 1) * lanes].astype(jnp.float32)

        @pl.loop(0, jrows)
        def _(i):
            r = p * jrows + i
            x = jnp.concatenate([fb[pl.ds(h * half + i, chan, stride=pxt), :] for h in range(2)], axis=1)
            xscale = jnp.concatenate([nc[u, 2]] * 2, axis=1)
            xshift = jnp.concatenate([nc[u, 3]] * 2, axis=1)
            upd = jnp.dot(wo[u], _norm_rows(x, xscale, xshift), preferred_element_type=jnp.float32)
            new = zb[r] + gb[r] * upd
            if u == 0:
                zb[r] = new
            else:
                zi[r] = new.T.reshape(chunks, n, jrows, chan).swapaxes(0, 1).reshape(cols, chan)

    def ocopy(p):
        at = pl.ds(p * jrows, jrows)
        return pltpu.make_async_copy(zi.at[at], o_hbm.at[at], osem.at[p])

    project(0)
    send_own(0)
    project(1)
    forward_far(0)
    send_own(1)
    prepare()
    forward_near(0)
    forward_opp(0)
    partner_all(0)
    outer(0, 0, blocks // 2)
    forward_far(1)
    outer(0, blocks // 2, blocks)
    zcopy.wait()
    mix(0)
    forward_near(1)
    piece_rows(0, ((0, 0), (jrows, 0)))
    turn(0)
    for t in (1, 0):
        for s in range(2):
            ab_send(0, t, 0, s)
    forward_opp(1)
    partner_all(1)
    outer(1, 0, blocks)
    mix(1)
    piece_rows(0, ((0, 1), (jrows, 1)))
    turn(1)
    for t in (1, 0):
        for s in range(2):
            ab_send(0, t, 1, s)
    for p in range(2):
        for s in range(2):
            ab_wait(0, 1, p, s)
    for p in range(2):
        ab_wait(0, 0, 0, p)
        ab_wait(0, 0, 1, p)
        x_out(p)
        x_send(0, p)
    sent(0)
    for p in range(2):
        x_wait(0, p)
        finish(0, p)
        piece_rows(1, ((p * jrows, 0), (p * jrows, 1)))
        turn(p)
        for t in range(2):
            for s in range(2):
                ab_send(1, t, p, s)
    x_sent(0)
    for t in range(2):
        for p in range(2):
            for s in range(2):
                ab_wait(1, t, p, s)
    x_in()
    for p in range(2):
        x_send(1, p)
    for p in range(2):
        x_wait(1, p)
        finish(1, p)
        ocopy(p).start()
    for p in range(2):
        ocopy(p).wait()
    sent(1)
    x_sent(1)
    for c in range(chunks):
        for h in (0, 1):
            for k, src in ((0, me), (1, me), (2, me), (3, left if h == 0 else right), (4, left if h == 0 else right),
                           (5, right if h == 0 else left), (6, opp)):
                send(c, h, src, k, part).wait_send()


def solution(mesh):
    row_spec = P(("data", "dap"), None, None)
    mask_spec = P(("data", "dap"), None)
    msa_spec = P(None, ("data", "dap"), None)
    replicated = P()

    def local_program(pair_loc, mask_loc, msa_loc, opm_norm, opm_proj, opm_out, opm_bias, tri_norm, tri_proj, tri_gate, tri_xnorm, tri_out):
        n = lax.axis_size("dap")
        rows, cols, chan = pair_loc.shape
        depth, _, mdim = msa_loc.shape
        odim = opm_proj.shape[1] // 2
        grp, chunks = 8, 2
        lanes = cols // chunks
        jrows = rows // chunks
        cown = chan // n
        vm = pl.BlockSpec(memory_space=pltpu.VMEM)
        hbm = pl.BlockSpec(memory_space=pl.ANY)
        f32, bf16 = jnp.float32, jnp.bfloat16
        dma = pltpu.SemaphoreType.DMA
        staged = max(4 * jrows * (chan + 8), depth // LANES * jrows * (odim + 8))
        return pl.pallas_call(
            functools.partial(_kernel, n),
            out_shape=jax.ShapeDtypeStruct(pair_loc.shape, f32),
            in_specs=[hbm, vm, hbm] + [vm] * 9,
            out_specs=hbm,
            scratch_shapes=[
                pltpu.VMEM((2, depth, grp, mdim), bf16),
                pltpu.VMEM((max(depth * grp, 2 * chan * (jrows + 8)), LANES), f32),
                pltpu.VMEM((rows * odim, depth), bf16),
                pltpu.VMEM((chunks, odim, lanes, depth), bf16),
                pltpu.VMEM((odim // 2, 2 * rows * odim // TILE, TILE, lanes), bf16),
                pltpu.VMEM((rows, cols, chan), f32),
                pltpu.VMEM((rows, chan, cols), f32),
                pltpu.VMEM((rows, chan, cols), f32),
                pltpu.VMEM((staged, LANES), f32),
                pltpu.VMEM((2, 2, 2, chan, jrows, lanes), bf16),
                pltpu.VMEM((2, 2, n, cown, jrows, lanes), bf16),
                pltpu.VMEM((2, 2, n, cown, jrows, lanes), bf16),
                pltpu.VMEM((2, n, cown, jrows, cols), bf16),
                pltpu.VMEM((2, chan, jrows, cols), bf16),
                pltpu.VMEM((rows, cols), f32),
                pltpu.VMEM((chan, odim * odim), bf16),
                pltpu.VMEM((2, 5 * chan, chan), bf16),
                pltpu.VMEM((2, chan, chan), bf16),
                pltpu.VMEM((2, 4, chan, lanes), f32),
                pltpu.VMEM((chan, lanes), f32),
                dma((2,)), dma((1,)), dma((2,)),
                dma((chunks, 2, 7)), dma((chunks, 2, n)),
                dma((2, 2, 2, 2, n)), dma((2, 2, 2, 2, n)),
                dma((2, 2, n)), dma((2, 2, n)),
            ],
            compiler_params=pltpu.CompilerParams(collective_id=0, has_side_effects=True, vmem_limit_bytes=63 * 1024 * 1024),
            name="pair_stack",
        )(pair_loc, mask_loc, msa_loc, opm_norm, opm_proj, opm_out, opm_bias.reshape(1, chan), tri_norm, tri_proj, tri_gate, tri_xnorm, tri_out)

    return jax.shard_map(local_program, mesh=mesh, in_specs=(row_spec, mask_spec, msa_spec) + (replicated,) * 9, out_specs=row_spec, check_vma=False)
```

time: 387 us -> 217 us (0.56)
  Pallas kernels: 0 us -> 210 us
  waiting for transfers between devices: 181 us -> 0 us
  local copies, waits for them, and re-layouts: 63.1 us -> 6.14 us
  matrix products: 54.9 us -> 0 us
  other arithmetic: 39.3 us -> 0 us
  starting transfers between devices: 30.5 us -> 0 us
  between operations: 14.1 us -> 0.01 us
    pallas_call x0 -> x1, Pallas kernels: none -> 210 us  [local_program(): pl.pallas_call(functools.partial(_kernel, n), out_shape=jax.ShapeDtypeStr...]
    all_to_all x6 -> x0, waiting for transfers between devices: 136 us -> none  [the longest x2 48.6 us: triangle_update(): right_chan = lax.all_to_all(right_act, 'dap', 0, 1, tiled=True)]
    dot_general x11 -> x0, matrix products: 54.9 us -> none  [the longest x1 19.7 us: outer_product_mean(): jnp.einsum('sip,sjq->ijpq', proj_all[:, :, :opm_dim], right_full, preferr...]
    all_gather x1 -> x0, waiting for transfers between devices: 44.9 us -> none  [outer_product_mean(): lax.all_gather(proj_all[:, :, opm_dim:], 'dap', axis=1, tiled=True)]
    convert_element_type x9 -> x0, local copies, waits for them, and re-layouts: 36.8 us -> none  [the longest x1 16.2 us: outer_product_mean(): outer_prod.astype(jnp.bfloat16)]
    all_to_all x6 -> x0, starting transfers between devices: 30.5 us -> none  [the longest x2 11.1 us: triangle_update(): right_chan = lax.all_to_all(right_act, 'dap', 0, 1, tiled=True)]
    reduce_sum x8 -> x0, other arithmetic: 23 us -> none  [the longest x5 16.5 us: norm_over(): chan_var = jnp.mean(centered * centered, axis=norm_axis, keepdims=True)]
    convert_element_type x6 -> x0, other arithmetic: 16.2 us -> none  [the longest x3 9.25 us: norm_over(): (centered * lax.rsqrt(chan_var + LN_EPS) * norm_scale + norm_shift).astyp...]
  transfers between devices with their start and end apart: 7 -> 0, of which waited for: 7 -> 0; matrix products, arithmetic and copies ran while one was open for 7% -> 0% of each run, Pallas kernels for 0% -> 0%
where the time goes in v3:
time: 217 us; the launch traced here: 216 us
  Pallas kernels  210 us (97%)
  local copies, waits for them, and re-layouts  6.14 us (3%)
    pallas_call x1, Pallas kernels, local_program(): pl.pallas_call(functools.partial(_kernel, n), out_shape=jax.ShapeDtypeStr...  210 us
    unnamed x2, local copies, waits for them, and re-layouts  6.14 us

profile of v3, /device:TPU:81, one launch (start us, length us, event | category | flops | bytes accessed | tf_op | source)
XLA Modules:
  0.0 216.5 jit_solution(14416530441684082730)
XLA Ops:
  0.0 1.5 copy.13.oproj_ref
  1.5 210.3 %pair_stack.1 = f32[32,256,128]{2,1,0:T(8,128)} custom-call(f32[32,256,128]{2,1,0:T(8,128)} %z_hbm.1, s32[32,256]{1,0:T(8,128)} %mask_ref.1, bf16[512,32,256]{2,1,0:T(8,128)(2,1)} %msa_hbm.1, f32[2,256]{1,0:T(2,128)} %onrm_ref.1, bf16[256,64]{1,0:T(8,128)(2,1)} %copy.13.oproj_ref, bf16[1024,128]{1,0:T(8,128)(2,1)} %oout_ref.1, f32[1,128]{1,0:T(1,128)} %bitcast.1, ...), custom_call_target="tpu_custom_call" | custom-call | tf_op jit(solution)/shard_map/pair_stack/pallas_call | solution.py:383
  211.8 4.7 %copy.15 = f32[32,256,128]{2,1,0:T(8,128)} copy(f32[32,256,128]{2,1,0:T(8,128)} %pair_stack.1) | data formatting | bytes 8388608

commit v4 on v3

--- a/solution.py
+++ b/solution.py
@@ -26,7 +26,7 @@
 
 def _kernel(n, z_hbm, mask_ref, msa_hbm, onrm_ref, oproj_ref, oout_ref, obias_ref, nrm_ref, proj_ref, gate_ref, xnrm_ref, out_ref, o_hbm,
             mb, fb, at_b, ball, obuf, zi, zb, gb, st, snd, ra, rb, xs, xr, mk, wt, wa, wo, nc, bc,
-            msem, zsem, osem, ss, rs, ss_ab, rs_ab, ss_x, rs_x):
+            msem, zsem, osem, ss, rs, ss_o, rs_o, ss_xo, rs_xo, ss_ab, rs_ab, ss_x, rs_x):
     me = lax.axis_index("dap")
     depth, grp, mdim = mb.shape[1:]
     rows, cols, chan = zi.shape
@@ -54,8 +54,14 @@
         pl.semaphore_signal(barrier, inc=1, device_id={"dap": lax.rem(me + s, n)}, device_id_type=MESH)
     pl.semaphore_wait(barrier, n - 1)
 
+    def slot(c, dev):
+        return lax.rem(dev + c * (n // 2), n)
+
+    def turned(v, c):
+        return v if c == 0 else jnp.concatenate([v[n // 2:], v[:n // 2]], axis=0)
+
     def block(c, h, src):
-        return ball.at[c, h * qh:(h + 1) * qh, pl.ds(pl.multiple_of(src * jrows, jrows), jrows)]
+        return ball.at[c, h * qh:(h + 1) * qh, pl.ds(pl.multiple_of(slot(c, src) * jrows, jrows), jrows)]
 
     def send(c, h, src, k, dst):
         return pltpu.make_async_remote_copy(
@@ -75,9 +81,9 @@
 
             @pl.loop(0, depth // sb)
             def _(b, g=g):
-                x = mb[g % 2, pl.ds(b * sb, sb)].astype(jnp.float32).reshape(sb * grp, mdim)
-                mean = jnp.mean(x, axis=1, keepdims=True)
-                cen = x - mean
+                x = mb[g % 2, pl.ds(b * sb, sb)].reshape(sb * grp, mdim)
+                mean = jnp.dot(x, jnp.ones((mdim, LANES), jnp.bfloat16), preferred_element_type=jnp.float32) * (1.0 / mdim)
+                cen = x.astype(jnp.float32) - jnp.concatenate([mean] * (mdim // LANES), axis=1)
                 var = jnp.mean(cen * cen, axis=1, keepdims=True)
                 y = (cen * lax.rsqrt(var + LN_EPS) * oscale + oshift).astype(jnp.bfloat16)
                 at = pl.ds(pl.multiple_of(b * (sb * grp), sb * grp), sb * grp)
@@ -97,7 +103,7 @@
         @pl.loop(0, odim, unroll=4)
         def _(q):
             for t in range(tiles):
-                ball[c, q, pl.ds(pl.multiple_of(me * jrows, jrows), jrows), t * LANES:(t + 1) * LANES] = (
+                ball[c, q, pl.ds(pl.multiple_of(slot(c, me) * jrows, jrows), jrows), t * LANES:(t + 1) * LANES] = (
                     st[pl.ds(t * (jrows * bst) + q, jrows, stride=bst), :].astype(jnp.bfloat16))
 
     def send_own(c):
@@ -147,14 +153,15 @@
             nt, w = rows * odim // TILE, odim // TILE
             rhs = jnp.stack([obuf[:, pl.ds(t * nt + i * w, w)] for t in range(2)], axis=1).reshape(odim * odim, lanes)
             upd = jnp.dot(wt[...], rhs, preferred_element_type=jnp.float32)
-            zt = zi[i].reshape(n, chunks, jrows, chan)[:, c].reshape(lanes, chan).T
+            zt = turned(zi[i].reshape(n, chunks, jrows, chan)[:, c], c).reshape(lanes, chan).T
             zb[i, :, c * lanes:(c + 1) * lanes] = zt + (upd + bc[...])
 
     def prepare():
         rid = lax.broadcasted_iota(jnp.int32, (cols, cols), 0)
         cid = lax.broadcasted_iota(jnp.int32, (cols, cols), 1)
         two = chunks * jrows
-        place = ((rid // jrows) % chunks) * lanes + (rid // two) * jrows + rid % jrows
+        piece = (rid // jrows) % chunks
+        place = piece * lanes + ((rid // two + piece * (n // 2)) % n) * jrows + rid % jrows
         perm = (cid == place).astype(jnp.float32).astype(jnp.bfloat16)
         mk[...] = jnp.dot(mask_ref[...].astype(jnp.float32).astype(jnp.bfloat16), perm, preferred_element_type=jnp.float32)
         bc[...] = _column(obias_ref[...], lanes)
@@ -199,64 +206,155 @@
 
     own = pl.ds(pl.multiple_of(me * cown, cown), cown)
 
-    def landing(u, t, p, s, src):
-        if u == 0:
-            return (rb if t else ra).at[p, s, src]
-        return obuf.at[t * 4 + p * 2 + s, pl.ds(pl.multiple_of(src * cown, cown), cown)]
-
-    def ab_copy(u, t, p, s, src, dst):
+    chip, core = me // 2, lax.rem(me, 2)
+    first, second = chip + 1 - 2 * lax.rem(chip, 2), n // 2 - 1 - chip
+    gchan, cslice = chan // 2, chan // 4
+    sides = (lax.rem((chip + 1) // 2, 2), chip // 2)
+
+    def mate(t, g):
+        return first if t == g else second
+
+    def o_copy(t, p, s, g, far, src_core, dst_core, sending):
+        other = 2 * (mate(t, g) if far else chip) + (dst_core if sending else src_core)
+        src = me if sending else other
+        buf = rb if t else ra
+        k = (2 if far else 0)
         return pltpu.make_async_remote_copy(
-            src_ref=snd.at[t, p, s, pl.ds(pl.multiple_of(dst * cown, cown), cown)], dst_ref=landing(u, t, p, s, src),
-            send_sem=ss_ab.at[u, t, p, s, dst], recv_sem=rs_ab.at[u, t, p, s, src],
+            src_ref=snd.at[t, p, s, pl.ds(pl.multiple_of(g * gchan + (dst_core if sending else core) * cslice, cslice), cslice)],
+            dst_ref=buf.at[g, p, slot(s, src)],
+            send_sem=ss_o.at[t, p, s, g, k + (dst_core if sending else 0)], recv_sem=rs_o.at[t, p, s, g, k + (core if sending else src_core)],
+            device_id={"dap": other}, device_id_type=MESH)
+
+    def o_send(t, p, s):
+        for g in range(2):
+            for c in range(2):
+                o_copy(t, p, s, g, True, core, c, True).start()
+            o_copy(t, p, s, g, False, core, 1 - core, True).start()
+            buf = rb if t else ra
+            buf[g, p, slot(s, me)] = snd[t, p, s, pl.ds(pl.multiple_of(g * gchan + core * cslice, cslice), cslice)]
+
+    def o_wait(t, p, s):
+        for g in range(2):
+            o_copy(t, p, s, g, False, 1 - core, core, False).wait_recv()
+            for c in range(2):
+                o_copy(t, p, s, g, True, c, core, False).wait_recv()
+
+    def o_sent():
+        for t in range(2):
+            for p in range(2):
+                for s in range(2):
+                    for g in range(2):
+                        for c in range(2):
+                            o_copy(t, p, s, g, True, core, c, True).wait_send()
+                        o_copy(t, p, s, g, False, core, 1 - core, True).wait_send()
+
+    def xo_copy(p, g, far, src_core, dst_core, sending):
+        other = 2 * (mate(0, g) if far else chip) + (dst_core if sending else src_core)
+        dst = other if sending else me
+        k = 2 if far else 0
+        return pltpu.make_async_remote_copy(
+            src_ref=xs.at[g, :, slot(p, dst)],
+            dst_ref=xr.at[p, sides[g], pl.ds((g * 2 + (core if sending else src_core)) * 2, 2)],
+            send_sem=ss_xo.at[p, g, k + (dst_core if sending else 0)], recv_sem=rs_xo.at[p, g, k + (core if sending else src_core)],
+            device_id={"dap": other}, device_id_type=MESH)
+
+    def xo_send(p):
+        for g in range(2):
+            for c in range(2):
+                xo_copy(p, g, True, core, c, True).start()
+            xo_copy(p, g, False, core, 1 - core, True).start()
+            xr[p, sides[g], pl.ds((g * 2 + core) * 2, 2)] = xs[g, :, slot(p, me)]
+
+    def xo_wait(p):
+        for g in range(2):
+            xo_copy(p, g, False, 1 - core, core, False).wait_recv()
+            for c in range(2):
+                xo_copy(p, g, True, c, core, False).wait_recv()
+
+    def xo_sent():
+        for p in range(2):
+            for g in range(2):
+                for c in range(2):
+                    xo_copy(p, g, True, core, c, True).wait_send()
+                xo_copy(p, g, False, core, 1 - core, True).wait_send()
+
+    def x_out(p):
+        for g in range(2):
+            at = [slot(p, 2 * w + c) for w in (chip, mate(0, g)) for c in range(2)]
+            for e in range(cslice // cown):
+                @pl.loop(0, cown, unroll=2)
+                def _(c, g=g, e=e, at=at):
+                    k = e * cown + c
+                    a = jnp.concatenate([jnp.concatenate([ra[g, h, d, k] for d in at], axis=0) for h in range(2)], axis=1)
+                    b = jnp.concatenate([rb[g, h, :, k].reshape(lanes, lanes) for h in range(2)], axis=1)
+                    x = lax.dot_general(a, b, (((1,), (1,)), ((), ())), preferred_element_type=jnp.float32).astype(jnp.bfloat16)
+                    for m, d in enumerate(at):
+                        xs[g, e, d, c] = x[m * jrows:(m + 1) * jrows]
+
+    def parts(p):
+        return ((0, cown),) if p == 0 else ((0, cown // 2), (cown // 2, cown // 2))
+
+    def landing(t, p, s, src, e):
+        lo, m = parts(p)[e]
+        return obuf.at[t * 4 + p * 2 + s, pl.ds(pl.multiple_of(src * cown, cown) + lo, m)]
+
+    def ab_copy(t, p, s, e, src, dst):
+        lo, m = parts(p)[e]
+        return pltpu.make_async_remote_copy(
+            src_ref=snd.at[t, p, s, pl.ds(pl.multiple_of(dst * cown, cown) + lo, m)], dst_ref=landing(t, p, s, src, e),
+            send_sem=ss_ab.at[t, p, s, e, dst], recv_sem=rs_ab.at[t, p, s, e, src],
             device_id={"dap": dst}, device_id_type=MESH)
 
-    def ab_send(u, t, p, s):
+    def ab_send(p, e):
+        lo, m = parts(p)[e]
+        for t in range(2):
+            for s in range(2):
+                for d in range(1, n):
+                    ab_copy(t, p, s, e, me, lax.rem(me + d, n)).start()
+                obuf[t * 4 + p * 2 + s, pl.ds(pl.multiple_of(me * cown, cown) + lo, m)] = snd[t, p, s, pl.ds(pl.multiple_of(me * cown, cown) + lo, m)]
+
+    def ab_wait(p, e):
+        for t in range(2):
+            for s in range(2):
+                for d in range(1, n):
+                    ab_copy(t, p, s, e, lax.rem(me + d, n), me).wait_recv()
+
+    def ab_sent():
+        for p in range(2):
+            for e in range(len(parts(p))):
+                for t in range(2):
+                    for s in range(2):
+                        for d in range(1, n):
+                            ab_copy(t, p, s, e, me, lax.rem(me + d, n)).wait_send()
+
+    hown = cown // 2
+
+    def x_copy(p, e, src, dst):
+        at = pl.ds(e * hown, hown)
+        return pltpu.make_async_remote_copy(
+            src_ref=xs.at[p, :, dst, at], dst_ref=xr.at[p, :, src, at],
+            send_sem=ss_x.at[p, e, dst], recv_sem=rs_x.at[p, e, src],
+            device_id={"dap": dst}, device_id_type=MESH)
+
+    def x_send(p, e):
         for d in range(1, n):
-            ab_copy(u, t, p, s, me, lax.rem(me + d, n)).start()
-        landing(u, t, p, s, me)[...] = snd[t, p, s, own]
-
-    def ab_wait(u, t, p, s):
-        for d in range(1, n):
-            ab_copy(u, t, p, s, lax.rem(me + d, n), me).wait_recv()
-
-    def x_copy(u, p, src, dst):
-        return pltpu.make_async_remote_copy(
-            src_ref=xs.at[p, dst], dst_ref=xr.at[p, pl.ds(pl.multiple_of(src * cown, cown), cown)],
-            send_sem=ss_x.at[u, p, dst], recv_sem=rs_x.at[u, p, src],
-            device_id={"dap": dst}, device_id_type=MESH)
-
-    def x_send(u, p):
-        for d in range(1, n):
-            x_copy(u, p, me, lax.rem(me + d, n)).start()
-        xr[p, own] = xs[p, me]
-
-    def x_wait(u, p):
-        for d in range(1, n):
-            x_copy(u, p, lax.rem(me + d, n), me).wait_recv()
-
-    def sent(u):
-        for d in range(1, n):
-            dst = lax.rem(me + d, n)
-            for t in range(2):
-                for p in range(2):
-                    for s in range(2):
-                        ab_copy(u, t, p, s, me, dst).wait_send()
-
-    def x_sent(u):
-        for d in range(1, n):
-            for p in range(2):
-                x_copy(u, p, me, lax.rem(me + d, n)).wait_send()
-
-    def x_out(p):
-        @pl.loop(0, cown)
-        def _(c):
-            a = jnp.concatenate([ra[h, p, :, c].reshape(lanes, lanes) for h in range(2)], axis=1)
-            b = jnp.concatenate([rb[h, :, :, c].reshape(cols, lanes) for h in range(2)], axis=1)
-            x = lax.dot_general(a, b, (((1,), (1,)), ((), ())), preferred_element_type=jnp.float32)
-            xs[p, :, c] = x.astype(jnp.bfloat16).reshape(n, jrows, cols)
-
-    def x_in():
-        @pl.loop(0, cown)
+            x_copy(p, e, me, lax.rem(me + d, n)).start()
+        at = slice(e * hown, (e + 1) * hown)
+        xr[p, :, me, at] = xs[p, :, me, at]
+
+    def x_wait(p):
+        for e in range(2):
+            for d in range(1, n):
+                x_copy(p, e, lax.rem(me + d, n), me).wait_recv()
+
+    def x_sent():
+        for p in range(2):
+            for e in range(2):
+                for d in range(1, n):
+                    x_copy(p, e, me, lax.rem(me + d, n)).wait_send()
+
+    def x_in(e):
+        @pl.loop(e * hown, (e + 1) * hown)
         def _(c):
             a, b = (jnp.concatenate([
                 jnp.concatenate([obuf[t * 4 + p * 2 + s, src * cown + c] for p in range(2) for src in range(n)], axis=0)
@@ -264,15 +362,24 @@
             x = lax.dot_general(a, b, (((0,), (0,)), ((), ())), preferred_element_type=jnp.float32)
             x = x.astype(jnp.bfloat16).reshape(2, n, jrows, cols)
             for p in range(2):
-                xs[p, :, c] = x[p]
+                v = turned(x[p], p)
+                for h in range(2):
+                    xs[p, h, :, c] = v[:, :, h * lanes:(h + 1) * lanes]
 
     def finish(u, p):
         half = chan * pxt
 
-        @pl.loop(0, chan, unroll=8)
-        def _(c):
-            for h in range(2):
-                fb[pl.ds(pl.multiple_of(h * half + c * pxt, 8), jrows), :] = xr[p, c, :, h * lanes:(h + 1) * lanes].astype(jnp.float32)
+        lane = lax.broadcasted_iota(jnp.int32, (jrows, lanes), 1) // (lanes // 4)
+        for k in range(n):
+            take = ((lane == 0) | (lane == 3)) if k < n // 2 else (lane < 2)
+
+            @pl.loop(0, cown, unroll=8)
+            def _(c, k=k, take=take):
+                x0, x1 = (xr[p, h, k, c].astype(jnp.float32) for h in range(2))
+                if u == 0:
+                    x0, x1 = jnp.where(take, x0, x1), jnp.where(take, x1, x0)
+                for h, x in enumerate((x0, x1)):
+                    fb[pl.ds(pl.multiple_of(h * half + (k * cown + c) * pxt, 8), jrows), :] = x
 
         @pl.loop(0, jrows)
         def _(i):
@@ -285,7 +392,8 @@
             if u == 0:
                 zb[r] = new
             else:
-                zi[r] = new.T.reshape(chunks, n, jrows, chan).swapaxes(0, 1).reshape(cols, chan)
+                new = new.T.reshape(chunks, n, jrows, chan)
+                zi[r] = jnp.stack([turned(new[c], c) for c in range(chunks)], axis=1).reshape(cols, chan)
 
     def ocopy(p):
         at = pl.ds(p * jrows, jrows)
@@ -310,7 +418,7 @@
     turn(0)
     for t in (1, 0):
         for s in range(2):
-            ab_send(0, t, 0, s)
+            o_send(t, 0, s)
     forward_opp(1)
     partner_all(1)
     outer(1, 0, blocks)
@@ -319,40 +427,38 @@
     turn(1)
     for t in (1, 0):
         for s in range(2):
-            ab_send(0, t, 1, s)
+            o_send(t, 1, s)
     for p in range(2):
         for s in range(2):
-            ab_wait(0, 1, p, s)
+            o_wait(1, p, s)
     for p in range(2):
-        ab_wait(0, 0, 0, p)
-        ab_wait(0, 0, 1, p)
+        o_wait(0, 0, p)
+        o_wait(0, 1, p)
         x_out(p)
-        x_send(0, p)
-    sent(0)
+        xo_send(p)
+    o_sent()
     for p in range(2):
-        x_wait(0, p)
+        xo_wait(p)
         finish(0, p)
         piece_rows(1, ((p * jrows, 0), (p * jrows, 1)))
         turn(p)
-        for t in range(2):
-            for s in range(2):
-                ab_send(1, t, p, s)
-    x_sent(0)
-    for t in range(2):
+        for e in range(len(parts(p))):
+            ab_send(p, e)
+    xo_sent()
+    ab_wait(0, 0)
+    for e in range(2):
+        ab_wait(1, e)
+        x_in(e)
         for p in range(2):
-            for s in range(2):
-                ab_wait(1, t, p, s)
-    x_in()
+            x_send(p, e)
     for p in range(2):
-        x_send(1, p)
-    for p in range(2):
-        x_wait(1, p)
+        x_wait(p)
         finish(1, p)
         ocopy(p).start()
     for p in range(2):
         ocopy(p).wait()
-    sent(1)
-    x_sent(1)
+    ab_sent()
+    x_sent()
     for c in range(chunks):
         for h in (0, 1):
             for k, src in ((0, me), (1, me), (2, me), (3, left if h == 0 else right), (4, left if h == 0 else right),
@@ -396,10 +502,10 @@
                 pltpu.VMEM((rows, chan, cols), f32),
                 pltpu.VMEM((staged, LANES), f32),
                 pltpu.VMEM((2, 2, 2, chan, jrows, lanes), bf16),
+                pltpu.VMEM((2, 2, n, chan // 4, jrows, lanes), bf16),
+                pltpu.VMEM((2, 2, n, chan // 4, jrows, lanes), bf16),
                 pltpu.VMEM((2, 2, n, cown, jrows, lanes), bf16),
                 pltpu.VMEM((2, 2, n, cown, jrows, lanes), bf16),
-                pltpu.VMEM((2, n, cown, jrows, cols), bf16),
-                pltpu.VMEM((2, chan, jrows, cols), bf16),
                 pltpu.VMEM((rows, cols), f32),
                 pltpu.VMEM((chan, odim * odim), bf16),
                 pltpu.VMEM((2, 5 * chan, chan), bf16),
@@ -408,8 +514,8 @@
                 pltpu.VMEM((chan, lanes), f32),
                 dma((2,)), dma((1,)), dma((2,)),
                 dma((chunks, 2, 7)), dma((chunks, 2, n)),
-                dma((2, 2, 2, 2, n)), dma((2, 2, 2, 2, n)),
-                dma((2, 2, n)), dma((2, 2, n)),
+                dma((2, 2, 2, 2, 4)), dma((2, 2, 2, 2, 4)), dma((2, 2, 4)), dma((2, 2, 4)),
+                dma((2, 2, 2, 2, n)), dma((2, 2, 2, 2, n)), dma((2, 2, n)), dma((2, 2, n)),
             ],
             compiler_params=pltpu.CompilerParams(collective_id=0, has_side_effects=True, vmem_limit_bytes=63 * 1024 * 1024),
             name="pair_stack",

time: 217 us -> 209 us (0.963)
  Pallas kernels: 210 us -> 203 us
    pallas_call x1, Pallas kernels: 210 us -> 203 us  [local_program(): pl.pallas_call(functools.partial(_kernel, n), out_shape=jax.ShapeDtypeStr...]
where the time goes in v4:
time: 209 us
  Pallas kernels  203 us (97%)
  local copies, waits for them, and re-layouts  6.14 us (3%)
    pallas_call x1, Pallas kernels, local_program(): pl.pallas_call(functools.partial(_kernel, n), out_shape=jax.ShapeDtypeStr...  203 us
    unnamed x2, local copies, waits for them, and re-layouts  6.14 us

profile of v4, /device:TPU:81, one launch (start us, length us, event | category | flops | bytes accessed | tf_op | source)
XLA Modules:
  0.0 208.7 jit_solution(7725138950327539131)
XLA Ops:
  0.0 1.5 copy.13.oproj_ref
  1.5 202.6 %pair_stack.1 = f32[32,256,128]{2,1,0:T(8,128)} custom-call(f32[32,256,128]{2,1,0:T(8,128)} %z_hbm.1, s32[32,256]{1,0:T(8,128)} %mask_ref.1, bf16[512,32,256]{2,1,0:T(8,128)(2,1)} %msa_hbm.1, f32[2,256]{1,0:T(2,128)} %onrm_ref.1, bf16[256,64]{1,0:T(8,128)(2,1)} %copy.13.oproj_ref, bf16[1024,128]{1,0:T(8,128)(2,1)} %oout_ref.1, f32[1,128]{1,0:T(1,128)} %bitcast.1, ...), custom_call_target="tpu_custom_call" | custom-call | tf_op jit(solution)/shard_map/pair_stack/pallas_call | solution.py:489
  204.1 4.7 %copy.15 = f32[32,256,128]{2,1,0:T(8,128)} copy(f32[32,256,128]{2,1,0:T(8,128)} %pair_stack.1) | data formatting | bytes 8388608

commit v5 on v4

--- a/solution.py
+++ b/solution.py
@@ -26,18 +26,16 @@
 
 def _kernel(n, z_hbm, mask_ref, msa_hbm, onrm_ref, oproj_ref, oout_ref, obias_ref, nrm_ref, proj_ref, gate_ref, xnrm_ref, out_ref, o_hbm,
             mb, fb, at_b, ball, obuf, zi, zb, gb, st, snd, ra, rb, xs, xr, mk, wt, wa, wo, nc, bc,
-            msem, zsem, osem, ss, rs, ss_o, rs_o, ss_xo, rs_xo, ss_ab, rs_ab, ss_x, rs_x):
+            msem, zsem, osem, ss, rs, rf, ss_o, rs_o, ss_xo, rs_xo, ss_ab, rs_ab, ss_x, rs_x):
     me = lax.axis_index("dap")
     depth, grp, mdim = mb.shape[1:]
     rows, cols, chan = zi.shape
-    chunks, odim, lanes = ball.shape[:3]
-    jrows = lanes // n
+    chunks, lanes, jrows, odim = 2, cols // 2, rows // 2, ball.shape[3]
     groups = rows // grp
     per = jrows // grp
     qh = odim // 2
     cown = chan // n
     blocks = odim // 2
-    tiles = depth // LANES
     bst, pst, pxt = odim + 8, chan + 8, jrows + 8
     part = me + 1 - 2 * lax.rem(me, 2)
     right, left, opp = lax.rem(me + 2, n), lax.rem(me + n - 2, n), lax.rem(me + 4, n)
@@ -61,7 +59,7 @@
         return v if c == 0 else jnp.concatenate([v[n // 2:], v[:n // 2]], axis=0)
 
     def block(c, h, src):
-        return ball.at[c, h * qh:(h + 1) * qh, pl.ds(pl.multiple_of(slot(c, src) * jrows, jrows), jrows)]
+        return ball.at[c, h, slot(c, src)]
 
     def send(c, h, src, k, dst):
         return pltpu.make_async_remote_copy(
@@ -71,31 +69,40 @@
     def arrived(c, h, src):
         send(c, h, src, 0, part).wait_recv()
 
+    def far(c, h, src, k, dst):
+        at = ball.at[c, h, slot(c, src), k * qh:(k + 1) * qh]
+        return pltpu.make_async_remote_copy(
+            src_ref=at, dst_ref=at, send_sem=ss.at[c, h, 6 + k], recv_sem=rf.at[c, h, k],
+            device_id={"dap": dst}, device_id_type=MESH)
+
     oscale, oshift = onrm_ref[0:1, :], onrm_ref[1:2, :]
     sb = 64
-
-    def project(c):
+    hdep = depth // 2
+    tiles = hdep // LANES
+
+    def project(c, h):
         for k in range(per):
             g = c * per + k
-            mcopy(g).wait()
-
-            @pl.loop(0, depth // sb)
+            if h == 0:
+                mcopy(g).wait()
+
+            @pl.loop(0, hdep // sb)
             def _(b, g=g):
-                x = mb[g % 2, pl.ds(b * sb, sb)].reshape(sb * grp, mdim)
-                mean = jnp.dot(x, jnp.ones((mdim, LANES), jnp.bfloat16), preferred_element_type=jnp.float32) * (1.0 / mdim)
-                cen = x.astype(jnp.float32) - jnp.concatenate([mean] * (mdim // LANES), axis=1)
+                x = mb[g % 2, pl.ds(h * hdep + b * sb, sb)].astype(jnp.float32).reshape(sb * grp, mdim)
+                mean = jnp.mean(x, axis=1, keepdims=True)
+                cen = x - mean
                 var = jnp.mean(cen * cen, axis=1, keepdims=True)
                 y = (cen * lax.rsqrt(var + LN_EPS) * oscale + oshift).astype(jnp.bfloat16)
                 at = pl.ds(pl.multiple_of(b * (sb * grp), sb * grp), sb * grp)
-                fb[at, :2 * odim] = jnp.dot(y, oproj_ref[...], preferred_element_type=jnp.float32)
-            if g + 2 < groups:
+                fb[at, :2 * odim] = lax.dot_general(y, oproj_ref[...], (((1,), (1,)), ((), ())), preferred_element_type=jnp.float32)
+            if h == 1 and g + 2 < groups:
                 mcopy(g + 2).start()
 
             @pl.loop(0, grp)
             def _(i, g=g, k=k):
-                v = fb[pl.ds(i, depth, stride=grp), :].T
+                v = fb[pl.ds(i, hdep, stride=grp), :].T
                 r = g * grp + i
-                at_b[pl.ds(pl.multiple_of(r * odim, odim), odim), :] = v[:odim].astype(jnp.bfloat16)
+                at_b[pl.ds(pl.multiple_of(r * odim, odim), odim), h * hdep:(h + 1) * hdep] = v[:odim].astype(jnp.bfloat16)
                 for t in range(tiles):
                     row = pl.multiple_of(t * (jrows * bst) + (k * grp + i) * bst, 8)
                     st[pl.ds(row, odim), :] = v[odim:2 * odim, t * LANES:(t + 1) * LANES]
@@ -103,34 +110,24 @@
         @pl.loop(0, odim, unroll=4)
         def _(q):
             for t in range(tiles):
-                ball[c, q, pl.ds(pl.multiple_of(slot(c, me) * jrows, jrows), jrows), t * LANES:(t + 1) * LANES] = (
+                ball[c, h, slot(c, me), q, :, t * LANES:(t + 1) * LANES] = (
                     st[pl.ds(t * (jrows * bst) + q, jrows, stride=bst), :].astype(jnp.bfloat16))
 
-    def send_own(c):
-        for h in (0, 1):
-            send(c, h, me, 0, right).start()
-            send(c, 1 - h, me, 1, left).start()
-        for h in (0, 1):
-            send(c, h, me, 2, part).start()
-
-    def forward_far(c):
-        arrived(c, 0, left)
-        send(c, 0, left, 3, right).start()
-        send(c, 0, left, 4, part).start()
-        arrived(c, 1, right)
-        send(c, 1, right, 3, left).start()
-        send(c, 1, right, 4, part).start()
-
-    def forward_near(c):
-        arrived(c, 1, left)
-        send(c, 1, left, 5, part).start()
-        arrived(c, 0, right)
-        send(c, 0, right, 5, part).start()
+    def send_own(c, h):
+        for k, dst in enumerate((right, left, part)):
+            send(c, h, me, k, dst).start()
+
+    def forward_far(c, h):
+        for k, (src, dst) in enumerate(((left, right), (right, left))):
+            arrived(c, h, src)
+            far(c, h, src, k, dst).start()
+            send(c, h, src, 3 + k, part).start()
 
     def forward_opp(c):
         for h in (0, 1):
-            arrived(c, h, opp)
-            send(c, h, opp, 6, part).start()
+            for k in (0, 1):
+                far(c, h, opp, k, part).wait_recv()
+            send(c, h, opp, 5, part).start()
 
     def partner_all(c):
         for d in (0, 2, 4, 6):
@@ -140,7 +137,7 @@
     def outer(c, lo, hi):
         @pl.loop(lo, hi)
         def _(b):
-            rhs = ball[c, pl.ds(b * 2, 2)].reshape(2 * lanes, depth)
+            rhs = jnp.concatenate([jnp.concatenate([ball[c, h, :, b * 2 + t].reshape(lanes, hdep) for h in range(2)], axis=1) for t in range(2)], axis=0)
             o = lax.dot_general(at_b[...], rhs, (((1,), (1,)), ((), ())), preferred_element_type=jnp.float32)
             o = (o * (1.0 / depth)).astype(jnp.bfloat16)
             nt = rows * odim // TILE
@@ -181,10 +178,10 @@
             v = jnp.concatenate([fb[pl.ds(b * m + k, odim, stride=odim), :] for k in range(m)], axis=0)
             wt[:, pl.ds(pl.multiple_of(b * LANES, LANES), LANES)] = v.T.astype(jnp.bfloat16)
 
-    def piece_rows(u, pieces):
-        @pl.loop(0, jrows)
+    def piece_rows(u, steps, pieces):
+        @pl.loop(0, steps)
         def _(i):
-            at = [(r0 + i, h * lanes) for r0, h in pieces]
+            at = [(r0 + i, h * lanes) for r0, h, _, _ in pieces]
             z = jnp.concatenate([zb[r, :, h:h + lanes] for r, h in at], axis=1)
             m = jnp.concatenate([mk[pl.ds(r, 1), :][:, h:h + lanes] for r, h in at], axis=1)
             scale = jnp.concatenate([nc[u, 0]] * 2, axis=1)
@@ -195,13 +192,14 @@
             for s, (r, h) in enumerate(at):
                 gb[r, :, h:h + lanes] = g[:, s * lanes:(s + 1) * lanes]
                 for t in range(2):
-                    st[pl.ds(pl.multiple_of((t * 2 + s) * (jrows * pst) + i * pst, 8), chan), :] = ab[t][:, s * lanes:(s + 1) * lanes]
-
-    def turn(p):
+                    row = pl.multiple_of((t * 2 + pieces[s][2]) * (jrows * pst) + (i + pieces[s][3]) * pst, 8)
+                    st[pl.ds(row, chan), :] = ab[t][:, s * lanes:(s + 1) * lanes]
+
+    def turn(p, which=(0, 1)):
         @pl.loop(0, chan, unroll=8)
         def _(c):
             for t in range(2):
-                for s in range(2):
+                for s in which:
                     snd[t, p, s, c] = st[pl.ds((t * 2 + s) * (jrows * pst) + c, jrows, stride=pst), :].astype(jnp.bfloat16)
 
     own = pl.ds(pl.multiple_of(me * cown, cown), cown)
@@ -305,10 +303,10 @@
             send_sem=ss_ab.at[t, p, s, e, dst], recv_sem=rs_ab.at[t, p, s, e, src],
             device_id={"dap": dst}, device_id_type=MESH)
 
-    def ab_send(p, e):
+    def ab_send(p, e, which=(0, 1)):
         lo, m = parts(p)[e]
-        for t in range(2):
-            for s in range(2):
+        for s in which:
+            for t in range(2):
                 for d in range(1, n):
                     ab_copy(t, p, s, e, me, lax.rem(me + d, n)).start()
                 obuf[t * 4 + p * 2 + s, pl.ds(pl.multiple_of(me * cown, cown) + lo, m)] = snd[t, p, s, pl.ds(pl.multiple_of(me * cown, cown) + lo, m)]
@@ -366,9 +364,9 @@
                 for h in range(2):
                     xs[p, h, :, c] = v[:, :, h * lanes:(h + 1) * lanes]
 
-    def finish(u, p):
-        half = chan * pxt
-
+    half = chan * pxt
+
+    def stage(u, p):
         lane = lax.broadcasted_iota(jnp.int32, (jrows, lanes), 1) // (lanes // 4)
         for k in range(n):
             take = ((lane == 0) | (lane == 3)) if k < n // 2 else (lane < 2)
@@ -381,40 +379,44 @@
                 for h, x in enumerate((x0, x1)):
                     fb[pl.ds(pl.multiple_of(h * half + (k * cown + c) * pxt, 8), jrows), :] = x
 
-        @pl.loop(0, jrows)
+    def finish(u, p, steps, pieces):
+        @pl.loop(0, steps)
         def _(i):
-            r = p * jrows + i
-            x = jnp.concatenate([fb[pl.ds(h * half + i, chan, stride=pxt), :] for h in range(2)], axis=1)
+            at = [(p * jrows + r0 + i, h * lanes) for r0, h in pieces]
+            x = jnp.concatenate([fb[pl.ds(h * half + r0 + i, chan, stride=pxt), :] for r0, h in pieces], axis=1)
             xscale = jnp.concatenate([nc[u, 2]] * 2, axis=1)
             xshift = jnp.concatenate([nc[u, 3]] * 2, axis=1)
             upd = jnp.dot(wo[u], _norm_rows(x, xscale, xshift), preferred_element_type=jnp.float32)
-            new = zb[r] + gb[r] * upd
+            new = [zb[r, :, h:h + lanes] + gb[r, :, h:h + lanes] * upd[:, k * lanes:(k + 1) * lanes] for k, (r, h) in enumerate(at)]
             if u == 0:
-                zb[r] = new
+                for (r, h), v in zip(at, new):
+                    zb[r, :, h:h + lanes] = v
             else:
-                new = new.T.reshape(chunks, n, jrows, chan)
-                zi[r] = jnp.stack([turned(new[c], c) for c in range(chunks)], axis=1).reshape(cols, chan)
+                zi[at[0][0]] = jnp.stack([turned(v.T.reshape(n, jrows, chan), c) for c, v in enumerate(new)], axis=1).reshape(cols, chan)
 
     def ocopy(p):
         at = pl.ds(p * jrows, jrows)
         return pltpu.make_async_copy(zi.at[at], o_hbm.at[at], osem.at[p])
 
-    project(0)
-    send_own(0)
-    project(1)
-    forward_far(0)
-    send_own(1)
+    project(0, 0)
+    send_own(0, 0)
+    project(0, 1)
+    send_own(0, 1)
+    project(1, 0)
+    forward_far(0, 0)
+    project(1, 1)
     prepare()
-    forward_near(0)
+    forward_far(0, 1)
+    send_own(1, 0)
+    send_own(1, 1)
     forward_opp(0)
     partner_all(0)
-    outer(0, 0, blocks // 2)
-    forward_far(1)
-    outer(0, blocks // 2, blocks)
+    outer(0, 0, blocks)
+    forward_far(1, 0)
     zcopy.wait()
     mix(0)
-    forward_near(1)
-    piece_rows(0, ((0, 0), (jrows, 0)))
+    forward_far(1, 1)
+    piece_rows(0, jrows, ((0, 0, 0, 0), (jrows, 0, 1, 0)))
     turn(0)
     for t in (1, 0):
         for s in range(2):
@@ -423,7 +425,7 @@
     partner_all(1)
     outer(1, 0, blocks)
     mix(1)
-    piece_rows(0, ((0, 1), (jrows, 1)))
+    piece_rows(0, jrows, ((0, 1, 0, 0), (jrows, 1, 1, 0)))
     turn(1)
     for t in (1, 0):
         for s in range(2):
@@ -437,13 +439,18 @@
         x_out(p)
         xo_send(p)
     o_sent()
+    hr = jrows // 2
     for p in range(2):
         xo_wait(p)
-        finish(0, p)
-        piece_rows(1, ((p * jrows, 0), (p * jrows, 1)))
-        turn(p)
-        for e in range(len(parts(p))):
-            ab_send(p, e)
+        stage(0, p)
+        for h in range(2):
+            finish(0, p, hr, ((0, h), (hr, h)))
+            piece_rows(1, hr, ((p * jrows, h, h, 0), (p * jrows + hr, h, h, hr)))
+            turn(p, (h,))
+            if p == 0:
+                ab_send(0, 0, (h,))
+    for e in range(2):
+        ab_send(1, e)
     xo_sent()
     ab_wait(0, 0)
     for e in range(2):
@@ -453,7 +460,8 @@
             x_send(p, e)
     for p in range(2):
         x_wait(p)
-        finish(1, p)
+        stage(1, p)
+        finish(1, p, jrows, ((0, 0), (0, 1)))
         ocopy(p).start()
     for p in range(2):
         ocopy(p).wait()
@@ -461,9 +469,10 @@
     x_sent()
     for c in range(chunks):
         for h in (0, 1):
-            for k, src in ((0, me), (1, me), (2, me), (3, left if h == 0 else right), (4, left if h == 0 else right),
-                           (5, right if h == 0 else left), (6, opp)):
+            for k, src in enumerate((me, me, me, left, right, opp)):
                 send(c, h, src, k, part).wait_send()
+            far(c, h, left, 0, right).wait_send()
+            far(c, h, right, 1, left).wait_send()
 
 
 def solution(mesh):
@@ -495,7 +504,7 @@
                 pltpu.VMEM((2, depth, grp, mdim), bf16),
                 pltpu.VMEM((max(depth * grp, 2 * chan * (jrows + 8)), LANES), f32),
                 pltpu.VMEM((rows * odim, depth), bf16),
-                pltpu.VMEM((chunks, odim, lanes, depth), bf16),
+                pltpu.VMEM((chunks, 2, n, odim, jrows, depth // 2), bf16),
                 pltpu.VMEM((odim // 2, 2 * rows * odim // TILE, TILE, lanes), bf16),
                 pltpu.VMEM((rows, cols, chan), f32),
                 pltpu.VMEM((rows, chan, cols), f32),
@@ -513,12 +522,12 @@
                 pltpu.VMEM((2, 4, chan, lanes), f32),
                 pltpu.VMEM((chan, lanes), f32),
                 dma((2,)), dma((1,)), dma((2,)),
-                dma((chunks, 2, 7)), dma((chunks, 2, n)),
+                dma((chunks, 2, 8)), dma((chunks, 2, n)), dma((chunks, 2, 2)),
                 dma((2, 2, 2, 2, 4)), dma((2, 2, 2, 2, 4)), dma((2, 2, 4)), dma((2, 2, 4)),
                 dma((2, 2, 2, 2, n)), dma((2, 2, 2, 2, n)), dma((2, 2, n)), dma((2, 2, n)),
             ],
             compiler_params=pltpu.CompilerParams(collective_id=0, has_side_effects=True, vmem_limit_bytes=63 * 1024 * 1024),
             name="pair_stack",
-        )(pair_loc, mask_loc, msa_loc, opm_norm, opm_proj, opm_out, opm_bias.reshape(1, chan), tri_norm, tri_proj, tri_gate, tri_xnorm, tri_out)
+        )(pair_loc, mask_loc, msa_loc, opm_norm, opm_proj.T, opm_out, opm_bias.reshape(1, chan), tri_norm, tri_proj, tri_gate, tri_xnorm, tri_out)
 
     return jax.shard_map(local_program, mesh=mesh, in_specs=(row_spec, mask_spec, msa_spec) + (replicated,) * 9, out_specs=row_spec, check_vma=False)

time: 209 us -> 199 us (0.952)
  Pallas kernels: 203 us -> 194 us
    pallas_call x1, Pallas kernels: 203 us -> 194 us  [local_program(): pl.pallas_call(functools.partial(_kernel, n), out_shape=jax.ShapeDtypeStr...]
    unnamed x2 -> x1, local copies, waits for them, and re-layouts: 6.14 us -> 4.65 us
where the time goes in v5:
time: 199 us
  Pallas kernels  194 us (97%)
  local copies, waits for them, and re-layouts  4.65 us (2%)
    pallas_call x1, Pallas kernels, local_program(): pl.pallas_call(functools.partial(_kernel, n), out_shape=jax.ShapeDtypeStr...  194 us
    unnamed x1, local copies, waits for them, and re-layouts  4.65 us

profile of v5, /device:TPU:81, one launch (start us, length us, event | category | flops | bytes accessed | tf_op | source)
XLA Modules:
  0.0 198.9 jit_solution(3611240303388456939)
XLA Ops:
  0.0 194.3 %pair_stack.1 = f32[32,256,128]{2,1,0:T(8,128)} custom-call(f32[32,256,128]{2,1,0:T(8,128)} %z_hbm.1, s32[32,256]{1,0:T(8,128)} %mask_ref.1, bf16[512,32,256]{2,1,0:T(8,128)(2,1)} %msa_hbm.1, f32[2,256]{1,0:T(2,128)} %onrm_ref.1, bf16[64,256]{1,0:T(8,128)(2,1)} %bitcast.2, bf16[1024,128]{1,0:T(8,128)(2,1)} %oout_ref.1, f32[1,128]{1,0:T(1,128)} %bitcast.3, ...), custom_call_target="tpu_custom_call" | custom-call | tf_op jit(solution)/shard_map/pair_stack/pallas_call | solution.py:498
  194.3 4.7 %copy.14 = f32[32,256,128]{2,1,0:T(8,128)} copy(f32[32,256,128]{2,1,0:T(8,128)} %pair_stack.1) | data formatting | bytes 8388608

commit v6 on v5

--- a/solution.py
+++ b/solution.py
@@ -28,11 +28,12 @@
             mb, fb, at_b, ball, obuf, zi, zb, gb, st, snd, ra, rb, xs, xr, mk, wt, wa, wo, nc, bc,
             msem, zsem, osem, ss, rs, rf, ss_o, rs_o, ss_xo, rs_xo, ss_ab, rs_ab, ss_x, rs_x):
     me = lax.axis_index("dap")
-    depth, grp, mdim = mb.shape[1:]
+    depth, _, mdim = mb.shape
     rows, cols, chan = zi.shape
     chunks, lanes, jrows, odim = 2, cols // 2, rows // 2, ball.shape[3]
-    groups = rows // grp
+    grp = 8
     per = jrows // grp
+    mblocks = msem.shape[0]
     qh = odim // 2
     cown = chan // n
     blocks = odim // 2
@@ -41,12 +42,12 @@
     right, left, opp = lax.rem(me + 2, n), lax.rem(me + n - 2, n), lax.rem(me + 4, n)
 
     def mcopy(g):
-        return pltpu.make_async_copy(msa_hbm.at[:, pl.ds(g * grp, grp)], mb.at[g % 2], msem.at[g % 2])
-
-    mcopy(0).start()
-    mcopy(1).start()
+        at = pl.ds(g * (depth // mblocks), depth // mblocks)
+        return pltpu.make_async_copy(msa_hbm.at[at], mb.at[at], msem.at[g])
+
+    for g in range(mblocks):
+        mcopy(g).start()
     zcopy = pltpu.make_async_copy(z_hbm, zi, zsem.at[0])
-    zcopy.start()
     barrier = pltpu.get_barrier_semaphore()
     for s in range(1, n):
         pl.semaphore_signal(barrier, inc=1, device_id={"dap": lax.rem(me + s, n)}, device_id_type=MESH)
@@ -76,32 +77,34 @@
             device_id={"dap": dst}, device_id_type=MESH)
 
     oscale, oshift = onrm_ref[0:1, :], onrm_ref[1:2, :]
-    sb = 64
+    sb = 32
     hdep = depth // 2
     tiles = hdep // LANES
 
     def project(c, h):
+        section = hdep * grp
+        if c == 0:
+            for g in range(h * mblocks // 2, (h + 1) * mblocks // 2):
+                mcopy(g).wait()
+
+        @pl.loop(0, hdep // sb)
+        def _(b):
+            x = mb[pl.ds(h * hdep + b * sb, sb), c * jrows:(c + 1) * jrows].astype(jnp.float32).reshape(sb * jrows, mdim)
+            mean = jnp.mean(x, axis=1, keepdims=True)
+            cen = x - mean
+            var = jnp.mean(cen * cen, axis=1, keepdims=True)
+            y = (cen * lax.rsqrt(var + LN_EPS) * oscale + oshift).astype(jnp.bfloat16)
+            v = lax.dot_general(y, oproj_ref[...], (((1,), (1,)), ((), ())), preferred_element_type=jnp.float32)
+            v = v.reshape(sb, per, grp, 2 * odim)
+            for k in range(per):
+                at = pl.ds(pl.multiple_of(k * section + b * (sb * grp), sb * grp), sb * grp)
+                fb[at, :2 * odim] = v[:, k].reshape(sb * grp, 2 * odim)
+
         for k in range(per):
-            g = c * per + k
-            if h == 0:
-                mcopy(g).wait()
-
-            @pl.loop(0, hdep // sb)
-            def _(b, g=g):
-                x = mb[g % 2, pl.ds(h * hdep + b * sb, sb)].astype(jnp.float32).reshape(sb * grp, mdim)
-                mean = jnp.mean(x, axis=1, keepdims=True)
-                cen = x - mean
-                var = jnp.mean(cen * cen, axis=1, keepdims=True)
-                y = (cen * lax.rsqrt(var + LN_EPS) * oscale + oshift).astype(jnp.bfloat16)
-                at = pl.ds(pl.multiple_of(b * (sb * grp), sb * grp), sb * grp)
-                fb[at, :2 * odim] = lax.dot_general(y, oproj_ref[...], (((1,), (1,)), ((), ())), preferred_element_type=jnp.float32)
-            if h == 1 and g + 2 < groups:
-                mcopy(g + 2).start()
-
             @pl.loop(0, grp)
-            def _(i, g=g, k=k):
-                v = fb[pl.ds(i, hdep, stride=grp), :].T
-                r = g * grp + i
+            def _(i, k=k):
+                v = fb[pl.ds(k * section + i, hdep, stride=grp), :].T
+                r = (c * per + k) * grp + i
                 at_b[pl.ds(pl.multiple_of(r * odim, odim), odim), h * hdep:(h + 1) * hdep] = v[:odim].astype(jnp.bfloat16)
                 for t in range(tiles):
                     row = pl.multiple_of(t * (jrows * bst) + (k * grp + i) * bst, 8)
@@ -144,8 +147,8 @@
             for t in range(2):
                 obuf[b, t * nt:(t + 1) * nt] = o[:, t * lanes:(t + 1) * lanes].reshape(nt, TILE, lanes)
 
-    def mix(c):
-        @pl.loop(0, rows)
+    def mix(c, lo, hi):
+        @pl.loop(lo, hi, unroll=2)
         def _(i):
             nt, w = rows * odim // TILE, odim // TILE
             rhs = jnp.stack([obuf[:, pl.ds(t * nt + i * w, w)] for t in range(2)], axis=1).reshape(odim * odim, lanes)
@@ -402,6 +405,7 @@
     send_own(0, 0)
     project(0, 1)
     send_own(0, 1)
+    zcopy.start()
     project(1, 0)
     forward_far(0, 0)
     project(1, 1)
@@ -411,11 +415,13 @@
     send_own(1, 1)
     forward_opp(0)
     partner_all(0)
-    outer(0, 0, blocks)
+    outer(0, 0, blocks * 3 // 8)
     forward_far(1, 0)
+    outer(0, blocks * 3 // 8, blocks)
     zcopy.wait()
-    mix(0)
+    mix(0, 0, rows // 2)
     forward_far(1, 1)
+    mix(0, rows // 2, rows)
     piece_rows(0, jrows, ((0, 0, 0, 0), (jrows, 0, 1, 0)))
     turn(0)
     for t in (1, 0):
@@ -424,7 +430,7 @@
     forward_opp(1)
     partner_all(1)
     outer(1, 0, blocks)
-    mix(1)
+    mix(1, 0, rows)
     piece_rows(0, jrows, ((0, 1, 0, 0), (jrows, 1, 1, 0)))
     turn(1)
     for t in (1, 0):
@@ -486,7 +492,7 @@
         rows, cols, chan = pair_loc.shape
         depth, _, mdim = msa_loc.shape
         odim = opm_proj.shape[1] // 2
-        grp, chunks = 8, 2
+        chunks = 2
         lanes = cols // chunks
         jrows = rows // chunks
         cown = chan // n
@@ -501,8 +507,8 @@
             in_specs=[hbm, vm, hbm] + [vm] * 9,
             out_specs=hbm,
             scratch_shapes=[
-                pltpu.VMEM((2, depth, grp, mdim), bf16),
-                pltpu.VMEM((max(depth * grp, 2 * chan * (jrows + 8)), LANES), f32),
+                pltpu.VMEM((depth, rows, mdim), bf16),
+                pltpu.VMEM((max(depth // 2 * jrows, 2 * chan * (jrows + 8)), LANES), f32),
                 pltpu.VMEM((rows * odim, depth), bf16),
                 pltpu.VMEM((chunks, 2, n, odim, jrows, depth // 2), bf16),
                 pltpu.VMEM((odim // 2, 2 * rows * odim // TILE, TILE, lanes), bf16),
@@ -521,12 +527,12 @@
                 pltpu.VMEM((2, chan, chan), bf16),
                 pltpu.VMEM((2, 4, chan, lanes), f32),
                 pltpu.VMEM((chan, lanes), f32),
-                dma((2,)), dma((1,)), dma((2,)),
+                dma((8,)), dma((1,)), dma((2,)),
                 dma((chunks, 2, 8)), dma((chunks, 2, n)), dma((chunks, 2, 2)),
                 dma((2, 2, 2, 2, 4)), dma((2, 2, 2, 2, 4)), dma((2, 2, 4)), dma((2, 2, 4)),
                 dma((2, 2, 2, 2, n)), dma((2, 2, 2, 2, n)), dma((2, 2, n)), dma((2, 2, n)),
             ],
-            compiler_params=pltpu.CompilerParams(collective_id=0, has_side_effects=True, vmem_limit_bytes=63 * 1024 * 1024),
+            compiler_params=pltpu.CompilerParams(collective_id=0, has_side_effects=True, vmem_limit_bytes=67043328),
             name="pair_stack",
         )(pair_loc, mask_loc, msa_loc, opm_norm, opm_proj.T, opm_out, opm_bias.reshape(1, chan), tri_norm, tri_proj, tri_gate, tri_xnorm, tri_out)
 

time: 199 us -> 196 us (0.985)
  Pallas kernels: 194 us -> 191 us
    pallas_call x1, Pallas kernels: 194 us -> 191 us  [local_program(): pl.pallas_call(functools.partial(_kernel, n), out_shape=jax.ShapeDtypeStr...]
where the time goes in v6:
time: 196 us
  Pallas kernels  191 us (97%)
  local copies, waits for them, and re-layouts  4.65 us (2%)
    pallas_call x1, Pallas kernels, local_program(): pl.pallas_call(functools.partial(_kernel, n), out_shape=jax.ShapeDtypeStr...  191 us
    unnamed x1, local copies, waits for them, and re-layouts  4.65 us

profile of v6, /device:TPU:81, one launch (start us, length us, event | category | flops | bytes accessed | tf_op | source)
XLA Modules:
  0.0 195.6 jit_solution(10860630329705463443)
XLA Ops:
  0.0 190.9 %pair_stack.1 = f32[32,256,128]{2,1,0:T(8,128)} custom-call(f32[32,256,128]{2,1,0:T(8,128)} %z_hbm.1, s32[32,256]{1,0:T(8,128)} %mask_ref.1, bf16[512,32,256]{2,1,0:T(8,128)(2,1)} %msa_hbm.1, f32[2,256]{1,0:T(2,128)} %onrm_ref.1, bf16[64,256]{1,0:T(8,128)(2,1)} %bitcast.2, bf16[1024,128]{1,0:T(8,128)(2,1)} %oout_ref.1, f32[1,128]{1,0:T(1,128)} %bitcast.3, ...), custom_call_target="tpu_custom_call" | custom-call | tf_op jit(solution)/shard_map/pair_stack/pallas_call | solution.py:504
  190.9 4.7 %copy.14 = f32[32,256,128]{2,1,0:T(8,128)} copy(f32[32,256,128]{2,1,0:T(8,128)} %pair_stack.1) | data formatting | bytes 8388608

commit v7 on v6

--- a/solution.py
+++ b/solution.py
@@ -24,12 +24,13 @@
     return jnp.broadcast_to(row, (n, row.shape[1])).T
 
 
-def _kernel(n, z_hbm, mask_ref, msa_hbm, onrm_ref, oproj_ref, oout_ref, obias_ref, nrm_ref, proj_ref, gate_ref, xnrm_ref, out_ref, o_hbm,
+def _kernel(n, z_hbm, mask_hbm, msa_hbm, onrm_hbm, oproj_hbm, oout_hbm, obias_hbm, nrm_hbm, proj_hbm, gate_hbm, xnrm_hbm, out_hbm, o_hbm,
+            mask_ref, onrm_ref, oproj_ref, oout_ref, obias_ref, nrm_ref, proj_ref, gate_ref, xnrm_ref, out_ref,
             mb, fb, at_b, ball, obuf, zi, zb, gb, st, snd, ra, rb, xs, xr, mk, wt, wa, wo, nc, bc,
-            msem, zsem, osem, ss, rs, rf, ss_o, rs_o, ss_xo, rs_xo, ss_ab, rs_ab, ss_x, rs_x):
+            wsem, msem, zsem, osem, ss, rs, rf, ss_o, rs_o, ss_xo, rs_xo, ss_ab, rs_ab, ss_x, rs_x):
     me = lax.axis_index("dap")
     depth, _, mdim = mb.shape
-    rows, cols, chan = zi.shape
+    rows, chan, cols = zb.shape
     chunks, lanes, jrows, odim = 2, cols // 2, rows // 2, ball.shape[3]
     grp = 8
     per = jrows // grp
@@ -45,13 +46,21 @@
         at = pl.ds(g * (depth // mblocks), depth // mblocks)
         return pltpu.make_async_copy(msa_hbm.at[at], mb.at[at], msem.at[g])
 
+    smalls = [pltpu.make_async_copy(a, b, wsem.at[k]) for k, (a, b) in enumerate((
+        (onrm_hbm, onrm_ref), (oproj_hbm, oproj_ref), (mask_hbm, mask_ref), (oout_hbm, oout_ref), (obias_hbm, obias_ref),
+        (nrm_hbm, nrm_ref), (proj_hbm, proj_ref), (gate_hbm, gate_ref), (xnrm_hbm, xnrm_ref), (out_hbm, out_ref)))]
+    for copy in smalls[:2]:
+        copy.start()
     for g in range(mblocks):
         mcopy(g).start()
+    for copy in smalls[2:]:
+        copy.start()
     zcopy = pltpu.make_async_copy(z_hbm, zi, zsem.at[0])
     barrier = pltpu.get_barrier_semaphore()
     for s in range(1, n):
         pl.semaphore_signal(barrier, inc=1, device_id={"dap": lax.rem(me + s, n)}, device_id_type=MESH)
-    pl.semaphore_wait(barrier, n - 1)
+    for copy in smalls[:2]:
+        copy.wait()
 
     def slot(c, dev):
         return lax.rem(dev + c * (n // 2), n)
@@ -83,12 +92,10 @@
 
     def project(c, h):
         section = hdep * grp
-        if c == 0:
-            for g in range(h * mblocks // 2, (h + 1) * mblocks // 2):
-                mcopy(g).wait()
-
         @pl.loop(0, hdep // sb)
         def _(b):
+            if c == 0:
+                mcopy(h * (hdep // sb) + b).wait()
             x = mb[pl.ds(h * hdep + b * sb, sb), c * jrows:(c + 1) * jrows].astype(jnp.float32).reshape(sb * jrows, mdim)
             mean = jnp.mean(x, axis=1, keepdims=True)
             cen = x - mean
@@ -153,10 +160,12 @@
             nt, w = rows * odim // TILE, odim // TILE
             rhs = jnp.stack([obuf[:, pl.ds(t * nt + i * w, w)] for t in range(2)], axis=1).reshape(odim * odim, lanes)
             upd = jnp.dot(wt[...], rhs, preferred_element_type=jnp.float32)
-            zt = turned(zi[i].reshape(n, chunks, jrows, chan)[:, c], c).reshape(lanes, chan).T
+            zt = turned(zi[i, :, c], c).reshape(lanes, chan).T
             zb[i, :, c * lanes:(c + 1) * lanes] = zt + (upd + bc[...])
 
     def prepare():
+        for copy in smalls[2:]:
+            copy.wait()
         rid = lax.broadcasted_iota(jnp.int32, (cols, cols), 0)
         cid = lax.broadcasted_iota(jnp.int32, (cols, cols), 1)
         two = chunks * jrows
@@ -330,29 +339,31 @@
 
     hown = cown // 2
 
-    def x_copy(p, e, src, dst):
+    def x_copy(p, e, h, src, dst):
         at = pl.ds(e * hown, hown)
         return pltpu.make_async_remote_copy(
-            src_ref=xs.at[p, :, dst, at], dst_ref=xr.at[p, :, src, at],
-            send_sem=ss_x.at[p, e, dst], recv_sem=rs_x.at[p, e, src],
+            src_ref=xs.at[p, h, dst, at], dst_ref=xr.at[p, h, src, at],
+            send_sem=ss_x.at[p, e, h, dst], recv_sem=rs_x.at[p, e, h, src],
             device_id={"dap": dst}, device_id_type=MESH)
 
     def x_send(p, e):
-        for d in range(1, n):
-            x_copy(p, e, me, lax.rem(me + d, n)).start()
+        for h in range(2):
+            for d in range(1, n):
+                x_copy(p, e, h, me, lax.rem(me + d, n)).start()
         at = slice(e * hown, (e + 1) * hown)
         xr[p, :, me, at] = xs[p, :, me, at]
 
-    def x_wait(p):
+    def x_wait(p, h):
         for e in range(2):
             for d in range(1, n):
-                x_copy(p, e, lax.rem(me + d, n), me).wait_recv()
+                x_copy(p, e, h, lax.rem(me + d, n), me).wait_recv()
 
     def x_sent():
         for p in range(2):
             for e in range(2):
-                for d in range(1, n):
-                    x_copy(p, e, me, lax.rem(me + d, n)).wait_send()
+                for h in range(2):
+                    for d in range(1, n):
+                        x_copy(p, e, h, me, lax.rem(me + d, n)).wait_send()
 
     def x_in(e):
         @pl.loop(e * hown, (e + 1) * hown)
@@ -369,17 +380,17 @@
 
     half = chan * pxt
 
-    def stage(u, p):
+    def stage(u, p, which=(0, 1)):
         lane = lax.broadcasted_iota(jnp.int32, (jrows, lanes), 1) // (lanes // 4)
         for k in range(n):
             take = ((lane == 0) | (lane == 3)) if k < n // 2 else (lane < 2)
 
             @pl.loop(0, cown, unroll=8)
             def _(c, k=k, take=take):
-                x0, x1 = (xr[p, h, k, c].astype(jnp.float32) for h in range(2))
+                x = [xr[p, h, k, c].astype(jnp.float32) for h in which]
                 if u == 0:
-                    x0, x1 = jnp.where(take, x0, x1), jnp.where(take, x1, x0)
-                for h, x in enumerate((x0, x1)):
+                    x = [jnp.where(take, x[0], x[1]), jnp.where(take, x[1], x[0])]
+                for h, x in zip(which, x):
                     fb[pl.ds(pl.multiple_of(h * half + (k * cown + c) * pxt, 8), jrows), :] = x
 
     def finish(u, p, steps, pieces):
@@ -395,13 +406,16 @@
                 for (r, h), v in zip(at, new):
                     zb[r, :, h:h + lanes] = v
             else:
-                zi[at[0][0]] = jnp.stack([turned(v.T.reshape(n, jrows, chan), c) for c, v in enumerate(new)], axis=1).reshape(cols, chan)
-
-    def ocopy(p):
+                for (r, h), v in zip(at, new):
+                    c = h // lanes
+                    zi[r, :, c] = turned(v.T.reshape(n, jrows, chan), c)
+
+    def ocopy(p, h):
         at = pl.ds(p * jrows, jrows)
-        return pltpu.make_async_copy(zi.at[at], o_hbm.at[at], osem.at[p])
+        return pltpu.make_async_copy(zi.at[at, :, h], o_hbm.at[at, :, h], osem.at[p * 2 + h])
 
     project(0, 0)
+    pl.semaphore_wait(barrier, n - 1)
     send_own(0, 0)
     project(0, 1)
     send_own(0, 1)
@@ -419,13 +433,14 @@
     forward_far(1, 0)
     outer(0, blocks * 3 // 8, blocks)
     zcopy.wait()
-    mix(0, 0, rows // 2)
-    forward_far(1, 1)
-    mix(0, rows // 2, rows)
-    piece_rows(0, jrows, ((0, 0, 0, 0), (jrows, 0, 1, 0)))
-    turn(0)
-    for t in (1, 0):
-        for s in range(2):
+    hr = jrows // 2
+    for s in range(2):
+        mix(0, s * jrows, (s + 1) * jrows)
+        if s == 0:
+            forward_far(1, 1)
+        piece_rows(0, hr, ((s * jrows, 0, s, 0), (s * jrows + hr, 0, s, hr)))
+        turn(0, (s,))
+        for t in (1, 0):
             o_send(t, 0, s)
     forward_opp(1)
     partner_all(1)
@@ -445,7 +460,6 @@
         x_out(p)
         xo_send(p)
     o_sent()
-    hr = jrows // 2
     for p in range(2):
         xo_wait(p)
         stage(0, p)
@@ -465,12 +479,14 @@
         for p in range(2):
             x_send(p, e)
     for p in range(2):
-        x_wait(p)
-        stage(1, p)
-        finish(1, p, jrows, ((0, 0), (0, 1)))
-        ocopy(p).start()
+        for h in range(2):
+            x_wait(p, h)
+            stage(1, p, (h,))
+            finish(1, p, hr, ((0, h), (hr, h)))
+            ocopy(p, h).start()
     for p in range(2):
-        ocopy(p).wait()
+        for h in range(2):
+            ocopy(p, h).wait()
     ab_sent()
     x_sent()
     for c in range(chunks):
@@ -496,23 +512,24 @@
         lanes = cols // chunks
         jrows = rows // chunks
         cown = chan // n
-        vm = pl.BlockSpec(memory_space=pltpu.VMEM)
         hbm = pl.BlockSpec(memory_space=pl.ANY)
         f32, bf16 = jnp.float32, jnp.bfloat16
         dma = pltpu.SemaphoreType.DMA
         staged = max(4 * jrows * (chan + 8), depth // LANES * jrows * (odim + 8))
+        block = (rows, n, chunks, jrows, chan)
+        smalls = (mask_loc, opm_norm, opm_proj.T, opm_out, opm_bias.reshape(1, chan), tri_norm, tri_proj, tri_gate, tri_xnorm, tri_out)
         return pl.pallas_call(
             functools.partial(_kernel, n),
-            out_shape=jax.ShapeDtypeStruct(pair_loc.shape, f32),
-            in_specs=[hbm, vm, hbm] + [vm] * 9,
+            out_shape=jax.ShapeDtypeStruct(block, f32),
+            in_specs=[hbm] * 12,
             out_specs=hbm,
-            scratch_shapes=[
+            scratch_shapes=[pltpu.VMEM(a.shape, a.dtype) for a in smalls] + [
                 pltpu.VMEM((depth, rows, mdim), bf16),
                 pltpu.VMEM((max(depth // 2 * jrows, 2 * chan * (jrows + 8)), LANES), f32),
                 pltpu.VMEM((rows * odim, depth), bf16),
                 pltpu.VMEM((chunks, 2, n, odim, jrows, depth // 2), bf16),
                 pltpu.VMEM((odim // 2, 2 * rows * odim // TILE, TILE, lanes), bf16),
-                pltpu.VMEM((rows, cols, chan), f32),
+                pltpu.VMEM(block, f32),
                 pltpu.VMEM((rows, chan, cols), f32),
                 pltpu.VMEM((rows, chan, cols), f32),
                 pltpu.VMEM((staged, LANES), f32),
@@ -527,13 +544,13 @@
                 pltpu.VMEM((2, chan, chan), bf16),
                 pltpu.VMEM((2, 4, chan, lanes), f32),
                 pltpu.VMEM((chan, lanes), f32),
-                dma((8,)), dma((1,)), dma((2,)),
+                dma((10,)), dma((depth // 32,)), dma((1,)), dma((4,)),
                 dma((chunks, 2, 8)), dma((chunks, 2, n)), dma((chunks, 2, 2)),
                 dma((2, 2, 2, 2, 4)), dma((2, 2, 2, 2, 4)), dma((2, 2, 4)), dma((2, 2, 4)),
-                dma((2, 2, 2, 2, n)), dma((2, 2, 2, 2, n)), dma((2, 2, n)), dma((2, 2, n)),
+                dma((2, 2, 2, 2, n)), dma((2, 2, 2, 2, n)), dma((2, 2, 2, n)), dma((2, 2, 2, n)),
             ],
             compiler_params=pltpu.CompilerParams(collective_id=0, has_side_effects=True, vmem_limit_bytes=67043328),
             name="pair_stack",
-        )(pair_loc, mask_loc, msa_loc, opm_norm, opm_proj.T, opm_out, opm_bias.reshape(1, chan), tri_norm, tri_proj, tri_gate, tri_xnorm, tri_out)
+        )(pair_loc.reshape(block), mask_loc, msa_loc, *smalls[1:]).reshape(pair_loc.shape)
 
     return jax.shard_map(local_program, mesh=mesh, in_specs=(row_spec, mask_spec, msa_spec) + (replicated,) * 9, out_specs=row_spec, check_vma=False)

time: 196 us -> 192 us (0.980)
  Pallas kernels: 191 us -> 187 us
    pallas_call x1, Pallas kernels: 191 us -> 187 us  [local_program(): pl.pallas_call(functools.partial(_kernel, n), out_shape=jax.ShapeDtypeStr...]
where the time goes in v7:
time: 192 us
  Pallas kernels  187 us (97%)
  local copies, waits for them, and re-layouts  4.65 us (2%)
    pallas_call x1, Pallas kernels, local_program(): pl.pallas_call(functools.partial(_kernel, n), out_shape=jax.ShapeDtypeStr...  187 us
    unnamed x1, local copies, waits for them, and re-layouts  4.65 us

profile of v7, /device:TPU:81, one launch (start us, length us, event | category | flops | bytes accessed | tf_op | source)
XLA Modules:
  0.0 192.1 jit_solution(5705155270000124787)
XLA Ops:
  0.0 187.5 %pair_stack.1 = f32[32,8,2,16,128]{4,3,2,1,0:T(8,128)} custom-call(f32[32,8,2,16,128]{4,3,2,1,0:T(8,128)} %bitcast.5, s32[32,256]{1,0:T(8,128)} %mask_hbm.1, bf16[512,32,256]{2,1,0:T(8,128)(2,1)} %msa_hbm.1, f32[2,256]{1,0:T(2,128)} %onrm_hbm.1, bf16[64,256]{1,0:T(8,128)(2,1)} %bitcast.6, bf16[1024,128]{1,0:T(8,128)(2,1)} %oout_hbm.1, f32[1,128]{1,0:T(1,128)} %bitcast.7, ...), custom_call_target="tpu_custom_call" | custom-call | tf_op jit(solution)/shard_map/pair_stack/pallas_call | solution.py:521
  187.5 4.7 %copy.14 = f32[32,256,128]{2,1,0:T(8,128)} copy(f32[32,256,128]{2,1,0:T(8,128)} %bitcast.4) | data formatting | bytes 8388608

commit v8 on v7

--- a/solution.py
+++ b/solution.py
@@ -87,7 +87,8 @@
 
     oscale, oshift = onrm_ref[0:1, :], onrm_ref[1:2, :]
     sb = 32
-    hdep = depth // 2
+    pieces_d = ball.shape[1]
+    hdep = depth // pieces_d
     tiles = hdep // LANES
 
     def project(c, h):
@@ -134,20 +135,20 @@
             send(c, h, src, 3 + k, part).start()
 
     def forward_opp(c):
-        for h in (0, 1):
+        for h in range(pieces_d):
             for k in (0, 1):
                 far(c, h, opp, k, part).wait_recv()
             send(c, h, opp, 5, part).start()
 
     def partner_all(c):
         for d in (0, 2, 4, 6):
-            for h in (0, 1):
+            for h in range(pieces_d):
                 arrived(c, h, lax.rem(part + d, n))
 
     def outer(c, lo, hi):
         @pl.loop(lo, hi)
         def _(b):
-            rhs = jnp.concatenate([jnp.concatenate([ball[c, h, :, b * 2 + t].reshape(lanes, hdep) for h in range(2)], axis=1) for t in range(2)], axis=0)
+            rhs = jnp.concatenate([jnp.concatenate([ball[c, h, :, b * 2 + t].reshape(lanes, hdep) for h in range(pieces_d)], axis=1) for t in range(2)], axis=0)
             o = lax.dot_general(at_b[...], rhs, (((1,), (1,)), ((), ())), preferred_element_type=jnp.float32)
             o = (o * (1.0 / depth)).astype(jnp.bfloat16)
             nt = rows * odim // TILE
@@ -417,40 +418,45 @@
     project(0, 0)
     pl.semaphore_wait(barrier, n - 1)
     send_own(0, 0)
-    project(0, 1)
-    send_own(0, 1)
+    for h in range(1, pieces_d):
+        project(0, h)
+        send_own(0, h)
     zcopy.start()
-    project(1, 0)
-    forward_far(0, 0)
-    project(1, 1)
-    prepare()
-    forward_far(0, 1)
-    send_own(1, 0)
-    send_own(1, 1)
+    for h in range(pieces_d):
+        project(1, h)
+        if h == pieces_d - 1:
+            prepare()
+        forward_far(0, h)
+    for h in range(pieces_d):
+        send_own(1, h)
     forward_opp(0)
     partner_all(0)
     outer(0, 0, blocks * 3 // 8)
-    forward_far(1, 0)
+    for h in range(pieces_d // 2):
+        forward_far(1, h)
     outer(0, blocks * 3 // 8, blocks)
     zcopy.wait()
     hr = jrows // 2
     for s in range(2):
         mix(0, s * jrows, (s + 1) * jrows)
         if s == 0:
-            forward_far(1, 1)
+            for h in range(pieces_d // 2, pieces_d):
+                forward_far(1, h)
         piece_rows(0, hr, ((s * jrows, 0, s, 0), (s * jrows + hr, 0, s, hr)))
         turn(0, (s,))
         for t in (1, 0):
             o_send(t, 0, s)
-    forward_opp(1)
+        if s == 0:
+            forward_opp(1)
     partner_all(1)
     outer(1, 0, blocks)
-    mix(1, 0, rows)
-    piece_rows(0, jrows, ((0, 1, 0, 0), (jrows, 1, 1, 0)))
-    turn(1)
-    for t in (1, 0):
-        for s in range(2):
-            o_send(t, 1, s)
+    for s in range(2):
+        mix(1, s * jrows, (s + 1) * jrows)
+        piece_rows(0, hr, ((s * jrows, 1, s, 0), (s * jrows + hr, 1, s, hr)))
+        turn(1, (s,))
+        o_send(1, 1, s)
+    for s in range(2):
+        o_send(0, 1, s)
     for p in range(2):
         for s in range(2):
             o_wait(1, p, s)
@@ -490,7 +496,7 @@
     ab_sent()
     x_sent()
     for c in range(chunks):
-        for h in (0, 1):
+        for h in range(pieces_d):
             for k, src in enumerate((me, me, me, left, right, opp)):
                 send(c, h, src, k, part).wait_send()
             far(c, h, left, 0, right).wait_send()
@@ -525,9 +531,9 @@
             out_specs=hbm,
             scratch_shapes=[pltpu.VMEM(a.shape, a.dtype) for a in smalls] + [
                 pltpu.VMEM((depth, rows, mdim), bf16),
-                pltpu.VMEM((max(depth // 2 * jrows, 2 * chan * (jrows + 8)), LANES), f32),
+                pltpu.VMEM((max(depth // 4 * jrows, 2 * chan * (jrows + 8)), LANES), f32),
                 pltpu.VMEM((rows * odim, depth), bf16),
-                pltpu.VMEM((chunks, 2, n, odim, jrows, depth // 2), bf16),
+                pltpu.VMEM((chunks, 4, n, odim, jrows, depth // 4), bf16),
                 pltpu.VMEM((odim // 2, 2 * rows * odim // TILE, TILE, lanes), bf16),
                 pltpu.VMEM(block, f32),
                 pltpu.VMEM((rows, chan, cols), f32),
@@ -545,7 +551,7 @@
                 pltpu.VMEM((2, 4, chan, lanes), f32),
                 pltpu.VMEM((chan, lanes), f32),
                 dma((10,)), dma((depth // 32,)), dma((1,)), dma((4,)),
-                dma((chunks, 2, 8)), dma((chunks, 2, n)), dma((chunks, 2, 2)),
+                dma((chunks, 4, 8)), dma((chunks, 4, n)), dma((chunks, 4, 2)),
                 dma((2, 2, 2, 2, 4)), dma((2, 2, 2, 2, 4)), dma((2, 2, 4)), dma((2, 2, 4)),
                 dma((2, 2, 2, 2, n)), dma((2, 2, 2, 2, n)), dma((2, 2, 2, n)), dma((2, 2, 2, n)),
             ],

time: 192 us -> 195 us (1.016)
  Pallas kernels: 187 us -> 190 us
    pallas_call x1, Pallas kernels: 187 us -> 190 us  [local_program(): pl.pallas_call(functools.partial(_kernel, n), out_shape=jax.ShapeDtypeStr...]
where the time goes in v8:
time: 195 us; the launch traced here: 194 us
  Pallas kernels  190 us (97%)
  local copies, waits for them, and re-layouts  4.65 us (2%)
    pallas_call x1, Pallas kernels, local_program(): pl.pallas_call(functools.partial(_kernel, n), out_shape=jax.ShapeDtypeStr...  190 us
    unnamed x1, local copies, waits for them, and re-layouts  4.65 us

profile of v8, /device:TPU:81, one launch (start us, length us, event | category | flops | bytes accessed | tf_op | source)
XLA Modules:
  0.0 194.4 jit_solution(2229429472233152303)
XLA Ops:
  0.0 189.8 %pair_stack.1 = f32[32,8,2,16,128]{4,3,2,1,0:T(8,128)} custom-call(f32[32,8,2,16,128]{4,3,2,1,0:T(8,128)} %bitcast.5, s32[32,256]{1,0:T(8,128)} %mask_hbm.1, bf16[512,32,256]{2,1,0:T(8,128)(2,1)} %msa_hbm.1, f32[2,256]{1,0:T(2,128)} %onrm_hbm.1, bf16[64,256]{1,0:T(8,128)(2,1)} %bitcast.6, bf16[1024,128]{1,0:T(8,128)(2,1)} %oout_hbm.1, f32[1,128]{1,0:T(1,128)} %bitcast.7, ...), custom_call_target="tpu_custom_call" | custom-call | tf_op jit(solution)/shard_map/pair_stack/pallas_call | solution.py:527
  189.8 4.7 %copy.14 = f32[32,256,128]{2,1,0:T(8,128)} copy(f32[32,256,128]{2,1,0:T(8,128)} %bitcast.4) | data formatting | bytes 8388608

commit v9 on v8

--- a/solution.py
+++ b/solution.py
@@ -431,23 +431,21 @@
         send_own(1, h)
     forward_opp(0)
     partner_all(0)
-    outer(0, 0, blocks * 3 // 8)
-    for h in range(pieces_d // 2):
+    cuts = (0, blocks * 3 // 8, blocks * 11 // 16, blocks)
+    for h in range(pieces_d - 1):
+        outer(0, cuts[h], cuts[h + 1])
         forward_far(1, h)
-    outer(0, blocks * 3 // 8, blocks)
     zcopy.wait()
     hr = jrows // 2
     for s in range(2):
         mix(0, s * jrows, (s + 1) * jrows)
         if s == 0:
-            for h in range(pieces_d // 2, pieces_d):
-                forward_far(1, h)
+            forward_far(1, pieces_d - 1)
         piece_rows(0, hr, ((s * jrows, 0, s, 0), (s * jrows + hr, 0, s, hr)))
         turn(0, (s,))
         for t in (1, 0):
             o_send(t, 0, s)
-        if s == 0:
-            forward_opp(1)
+    forward_opp(1)
     partner_all(1)
     outer(1, 0, blocks)
     for s in range(2):

time: 195 us -> 193 us (0.990)
  Pallas kernels: 190 us -> 188 us
where the time goes in v9:
time: 193 us
  Pallas kernels  188 us (97%)
  local copies, waits for them, and re-layouts  4.65 us (2%)
    pallas_call x1, Pallas kernels, local_program(): pl.pallas_call(functools.partial(_kernel, n), out_shape=jax.ShapeDtypeStr...  188 us
    unnamed x1, local copies, waits for them, and re-layouts  4.65 us

profile of v9, /device:TPU:81, one launch (start us, length us, event | category | flops | bytes accessed | tf_op | source)
XLA Modules:
  0.0 193.1 jit_solution(7899119971205660082)
XLA Ops:
  0.0 188.4 %pair_stack.1 = f32[32,8,2,16,128]{4,3,2,1,0:T(8,128)} custom-call(f32[32,8,2,16,128]{4,3,2,1,0:T(8,128)} %bitcast.5, s32[32,256]{1,0:T(8,128)} %mask_hbm.1, bf16[512,32,256]{2,1,0:T(8,128)(2,1)} %msa_hbm.1, f32[2,256]{1,0:T(2,128)} %onrm_hbm.1, bf16[64,256]{1,0:T(8,128)(2,1)} %bitcast.6, bf16[1024,128]{1,0:T(8,128)(2,1)} %oout_hbm.1, f32[1,128]{1,0:T(1,128)} %bitcast.7, ...), custom_call_target="tpu_custom_call" | custom-call | tf_op jit(solution)/shard_map/pair_stack/pallas_call | solution.py:525
  188.4 4.7 %copy.14 = f32[32,256,128]{2,1,0:T(8,128)} copy(f32[32,256,128]{2,1,0:T(8,128)} %bitcast.4) | data formatting | bytes 8388608

commit v10 on v7

--- a/solution.py
+++ b/solution.py
@@ -445,12 +445,13 @@
     forward_opp(1)
     partner_all(1)
     outer(1, 0, blocks)
-    mix(1, 0, rows)
-    piece_rows(0, jrows, ((0, 1, 0, 0), (jrows, 1, 1, 0)))
-    turn(1)
-    for t in (1, 0):
-        for s in range(2):
-            o_send(t, 1, s)
+    for s in range(2):
+        mix(1, s * jrows, (s + 1) * jrows)
+        piece_rows(0, hr, ((s * jrows, 1, s, 0), (s * jrows + hr, 1, s, hr)))
+        turn(1, (s,))
+        o_send(1, 1, s)
+    for s in range(2):
+        o_send(0, 1, s)
     for p in range(2):
         for s in range(2):
             o_wait(1, p, s)
@@ -497,6 +498,35 @@
             far(c, h, right, 1, left).wait_send()
 
 
+def _carry_kernel(src_hbm, dst_hbm, buf, in_sem, out_sem):
+    pieces = in_sem.shape[0]
+    step = buf.shape[0] // pieces
+    at = [pl.ds(k * step, step) for k in range(pieces)]
+    reads = [pltpu.make_async_copy(src_hbm.at[a], buf.at[a], in_sem.at[k]) for k, a in enumerate(at)]
+    writes = [pltpu.make_async_copy(buf.at[a], dst_hbm.at[a], out_sem.at[k]) for k, a in enumerate(at)]
+    for copy in reads:
+        copy.start()
+    for read, write in zip(reads, writes):
+        read.wait()
+        write.start()
+    for copy in writes:
+        copy.wait()
+
+
+def _carry(v):
+    hbm = pl.BlockSpec(memory_space=pl.ANY)
+    pieces = 16
+    return pl.pallas_call(
+        _carry_kernel,
+        out_shape=jax.ShapeDtypeStruct(v.shape, v.dtype),
+        in_specs=[hbm],
+        out_specs=hbm,
+        scratch_shapes=[pltpu.VMEM(v.shape, v.dtype), pltpu.SemaphoreType.DMA((pieces,)), pltpu.SemaphoreType.DMA((pieces,))],
+        compiler_params=pltpu.CompilerParams(vmem_limit_bytes=60 * 1024 * 1024),
+        name="carry",
+    )(v)
+
+
 def solution(mesh):
     row_spec = P(("data", "dap"), None, None)
     mask_spec = P(("data", "dap"), None)
@@ -518,7 +548,7 @@
         staged = max(4 * jrows * (chan + 8), depth // LANES * jrows * (odim + 8))
         block = (rows, n, chunks, jrows, chan)
         smalls = (mask_loc, opm_norm, opm_proj.T, opm_out, opm_bias.reshape(1, chan), tri_norm, tri_proj, tri_gate, tri_xnorm, tri_out)
-        return pl.pallas_call(
+        out = pl.pallas_call(
             functools.partial(_kernel, n),
             out_shape=jax.ShapeDtypeStruct(block, f32),
             in_specs=[hbm] * 12,
@@ -551,6 +581,7 @@
             ],
             compiler_params=pltpu.CompilerParams(collective_id=0, has_side_effects=True, vmem_limit_bytes=67043328),
             name="pair_stack",
-        )(pair_loc.reshape(block), mask_loc, msa_loc, *smalls[1:]).reshape(pair_loc.shape)
+        )(pair_loc.reshape(block), mask_loc, msa_loc, *smalls[1:])
+        return _carry(out).reshape(pair_loc.shape)
 
     return jax.shard_map(local_program, mesh=mesh, in_specs=(row_spec, mask_spec, msa_spec) + (replicated,) * 9, out_specs=row_spec, check_vma=False)

time: 192 us -> 188 us (0.979)
  local copies, waits for them, and re-layouts: 4.65 us -> 0 us
    unnamed x1 -> x0, local copies, waits for them, and re-layouts: 4.65 us -> none
    pallas_call x0 -> x1, Pallas kernels: none -> 3.85 us  [_carry(): pl.pallas_call(_carry_kernel, out_shape=jax.ShapeDtypeStruct(v.shape, v.d...]
    pallas_call x1, Pallas kernels: 187 us -> 184 us  [local_program(): pl.pallas_call(functools.partial(_kernel, n), out_shape=jax.ShapeDtypeStr...]
where the time goes in v10:
time: 188 us
  Pallas kernels  188 us (100%)
    pallas_call x1, Pallas kernels, local_program(): pl.pallas_call(functools.partial(_kernel, n), out_shape=jax.ShapeDtypeStr...  184 us
    pallas_call x1, Pallas kernels, _carry(): pl.pallas_call(_carry_kernel, out_shape=jax.ShapeDtypeStruct(v.shape, v.d...  3.85 us

profile of v10, /device:TPU:81, one launch (start us, length us, event | category | flops | bytes accessed | tf_op | source)
XLA Modules:
  0.0 188.0 jit_solution(9799897526637173674)
XLA Ops:
  0.0 184.1 %pair_stack.1.src_hbm = f32[32,8,2,16,128]{4,3,2,1,0:T(8,128)} custom-call(f32[32,8,2,16,128]{4,3,2,1,0:T(8,128)} %bitcast.4, s32[32,256]{1,0:T(8,128)} %mask_hbm.1, bf16[512,32,256]{2,1,0:T(8,128)(2,1)} %msa_hbm.1, f32[2,256]{1,0:T(2,128)} %onrm_hbm.1, bf16[64,256]{1,0:T(8,128)(2,1)} %bitcast.5, bf16[1024,128]{1,0:T(8,128)(2,1)} %oout_hbm.1, ...), custom_call_target="tpu_custom_call" | custom-call | tf_op jit(solution)/shard_map/pair_stack/pallas_call | solution.py:551
  184.1 3.9 %carry.1 = f32[32,8,2,16,128]{4,3,2,1,0:T(8,128)} custom-call(f32[32,8,2,16,128]{4,3,2,1,0:T(8,128)} %pair_stack.1.src_hbm), custom_call_target="tpu_custom_call" | custom-call | tf_op jit(solution)/shard_map/carry/pallas_call | solution.py:519

commit v11 on v10

--- a/solution.py
+++ b/solution.py
@@ -144,15 +144,15 @@
             for h in (0, 1):
                 arrived(c, h, lax.rem(part + d, n))
 
-    def outer(c, lo, hi):
+    def outer(c, lo, hi, r0=0, nr=rows):
         @pl.loop(lo, hi)
         def _(b):
             rhs = jnp.concatenate([jnp.concatenate([ball[c, h, :, b * 2 + t].reshape(lanes, hdep) for h in range(2)], axis=1) for t in range(2)], axis=0)
-            o = lax.dot_general(at_b[...], rhs, (((1,), (1,)), ((), ())), preferred_element_type=jnp.float32)
+            o = lax.dot_general(at_b[r0 * odim:(r0 + nr) * odim], rhs, (((1,), (1,)), ((), ())), preferred_element_type=jnp.float32)
             o = (o * (1.0 / depth)).astype(jnp.bfloat16)
-            nt = rows * odim // TILE
+            nt, w = rows * odim // TILE, odim // TILE
             for t in range(2):
-                obuf[b, t * nt:(t + 1) * nt] = o[:, t * lanes:(t + 1) * lanes].reshape(nt, TILE, lanes)
+                obuf[b, t * nt + r0 * w:t * nt + (r0 + nr) * w] = o[:, t * lanes:(t + 1) * lanes].reshape(nr * w, TILE, lanes)
 
     def mix(c, lo, hi):
         @pl.loop(lo, hi, unroll=2)
@@ -444,14 +444,13 @@
             o_send(t, 0, s)
     forward_opp(1)
     partner_all(1)
-    outer(1, 0, blocks)
     for s in range(2):
+        outer(1, 0, blocks, s * jrows, jrows)
         mix(1, s * jrows, (s + 1) * jrows)
         piece_rows(0, hr, ((s * jrows, 1, s, 0), (s * jrows + hr, 1, s, hr)))
         turn(1, (s,))
-        o_send(1, 1, s)
-    for s in range(2):
-        o_send(0, 1, s)
+        for t in (1, 0):
+            o_send(t, 1, s)
     for p in range(2):
         for s in range(2):
             o_wait(1, p, s)

time: 188 us -> 189 us (level)
  no operation moved by 1% of the time
where the time goes in v11:
time: 189 us; the launch traced here: 188 us
  Pallas kernels  188 us (99%)
    pallas_call x1, Pallas kernels, local_program(): pl.pallas_call(functools.partial(_kernel, n), out_shape=jax.ShapeDtypeStr...  185 us
    pallas_call x1, Pallas kernels, _carry(): pl.pallas_call(_carry_kernel, out_shape=jax.ShapeDtypeStruct(v.shape, v.d...  3.85 us

profile of v11, /device:TPU:81, one launch (start us, length us, event | category | flops | bytes accessed | tf_op | source)
XLA Modules:
  0.0 188.5 jit_solution(17944592560552822864)
XLA Ops:
  0.0 184.6 %pair_stack.1.src_hbm = f32[32,8,2,16,128]{4,3,2,1,0:T(8,128)} custom-call(f32[32,8,2,16,128]{4,3,2,1,0:T(8,128)} %bitcast.4, s32[32,256]{1,0:T(8,128)} %mask_hbm.1, bf16[512,32,256]{2,1,0:T(8,128)(2,1)} %msa_hbm.1, f32[2,256]{1,0:T(2,128)} %onrm_hbm.1, bf16[64,256]{1,0:T(8,128)(2,1)} %bitcast.5, bf16[1024,128]{1,0:T(8,128)(2,1)} %oout_hbm.1, ...), custom_call_target="tpu_custom_call" | custom-call | tf_op jit(solution)/shard_map/pair_stack/pallas_call | solution.py:550
  184.6 3.9 %carry.1 = f32[32,8,2,16,128]{4,3,2,1,0:T(8,128)} custom-call(f32[32,8,2,16,128]{4,3,2,1,0:T(8,128)} %pair_stack.1.src_hbm), custom_call_target="tpu_custom_call" | custom-call | tf_op jit(solution)/shard_map/carry/pallas_call | solution.py:518
